TPU v7x, 8 devices: a whole 2x2x1 slice. The times are simulated.
8 devices in a mesh: nodes: 8 (over z, y, x, core).
Axes of the slice: x: 2, y: 2, z: 1, core: 2. Of those that a mesh axis runs over, the one named last changes fastest.
Arguments:
- adjacency: bfloat16 [16384, 16384], P('nodes')
- features: bfloat16 [16384, 128], P('nodes')
- w_one: float32 [128, 256], replicated
- w_two: float32 [256, 349], replicated
- labels: int32 [16384], P('nodes')
- label_mask: int32 [16384], P('nodes')
Outputs:
- output 1: float32 [], replicated
- output 2: float32 [128, 256], replicated
- output 3: float32 [256, 349], replicated
All inputs are finite; a program needn't handle non-finite values.
Results may differ from a plain program's by a relative error of at most 0.00157.
Values are sent between devices in bfloat16 or wider.
A program may use at most 1 GiB of HBM per device.

v0:
```python
import jax
import jax.numpy as jnp
from jax import lax
from jax.sharding import PartitionSpec as P


def contract_rows(left, right):
    return lax.dot_general(left, right, (((0,), (0,)), ((), ())), preferred_element_type=jnp.float32)


def solution(mesh):
    node_axis = mesh.axis_names[0]

    def local_step(adj_rows, feat_rows, w_one, w_two, label_rows, mask_rows):
        classes = w_two.shape[1]
        w_one_b = w_one.astype(jnp.bfloat16)
        w_two_b = w_two.astype(jnp.bfloat16)
        y_one = jnp.dot(feat_rows, w_one_b, preferred_element_type=jnp.float32).astype(jnp.bfloat16)
        y_one_all = lax.all_gather(y_one, node_axis, tiled=True)
        z_one = jnp.dot(adj_rows, y_one_all, preferred_element_type=jnp.float32)
        h_one = jnp.maximum(z_one, 0.0).astype(jnp.bfloat16)
        y_two = jnp.dot(h_one, w_two_b, preferred_element_type=jnp.float32).astype(jnp.bfloat16)
        y_two_all = lax.all_gather(y_two, node_axis, tiled=True)
        z_two = jnp.dot(adj_rows, y_two_all, preferred_element_type=jnp.float32)
        mask_f = mask_rows.astype(jnp.float32)
        label_count = lax.psum(jnp.sum(mask_f), node_axis)
        log_norm = jax.nn.logsumexp(z_two, axis=1)
        onehot = (label_rows[:, None] == jnp.arange(classes, dtype=jnp.int32)[None, :]).astype(jnp.float32)
        picked = jnp.sum(z_two * onehot, axis=1)
        loss_value = lax.psum(jnp.sum(mask_f * (log_norm - picked)), node_axis) / label_count
        soft_probs = jnp.exp(z_two - log_norm[:, None])
        g_two = ((soft_probs - onehot) * (mask_f / label_count)[:, None]).astype(jnp.bfloat16)
        part_y2 = contract_rows(adj_rows, g_two)
        grad_y2 = lax.psum_scatter(part_y2, node_axis, scatter_dimension=0, tiled=True).astype(jnp.bfloat16)
        grad_two = lax.psum(contract_rows(h_one, grad_y2), node_axis)
        grad_h1 = lax.dot_general(grad_y2, w_two_b, (((1,), (1,)), ((), ())), preferred_element_type=jnp.float32)
        grad_z1 = jnp.where(z_one > 0.0, grad_h1, 0.0).astype(jnp.bfloat16)
        part_y1 = contract_rows(adj_rows, grad_z1)
        grad_y1 = lax.psum_scatter(part_y1, node_axis, scatter_dimension=0, tiled=True).astype(jnp.bfloat16)
        grad_one = lax.psum(contract_rows(feat_rows, grad_y1), node_axis)
        return loss_value, grad_one, grad_two

    return jax.shard_map(local_step, mesh=mesh, in_specs=(P(node_axis, None), P(node_axis, None), P(None, None), P(None, None), P(node_axis), P(node_axis)), out_specs=(P(), P(None, None), P(None, None)), check_vma=False)
```

profile of v0, /device:TPU:0, one launch (start us, length us, event | category | flops | bytes accessed | tf_op | source)
XLA Modules:
  0.0 595.2 jit_solution(5487698621770288519)
XLA Ops:
  7.2 0.0 copy-start
  7.2 0.0 all-gather.3.cloned.1.call-start
  7.2 1.0 copy-done
  8.2 2.4 convolution_convert_fusion.1
  10.6 0.0 all-gather.3.cloned.1.call-update
  10.6 0.0 copy-start.1
  10.6 0.0 all-gather.5.cloned.1.call-start
  10.7 51.3 %all-gather.3.cloned.1.call-done = bf16[16384,256]{1,0:T(8,128)(2,1)} async-done(((bf16[2048,256]{1,0:T(8,128)(2,1)}), bf16[16384,256]{1,0:T(8,128)(2,1)}) %all-gather.3.cloned.1.call-update) | async-done | bytes 8388624 | tf_op jit(solution)/shard_map/all_gather | solution.py:19
  61.9 28.5 %fusion.25 = f32[256,2048]{1,0:T(8,128)S(1)} fusion(bf16[16384,256]{1,0:T(8,128)(2,1)} %all-gather.3.cloned.1.call-done, bf16[2048,16384]{1,0:T(8,128)(2,1)} %param.6), kind=kOutput, calls=%fused_computation.38 | convolution fusion | flops 17179869184 | bytes 77594624 | tf_op jit(solution)/shard_map/dot_general | solution.py:20
  90.5 0.0 copy-done.1
  90.5 2.0 convolution_convert_fusion
  92.4 0.0 all-gather.5.cloned.1.call-update
  92.5 0.0 copy-start.3
  92.5 0.0 reduce-scatter.3.cloned.1.call-start
  92.5 66.4 %all-gather.5.cloned.1.call-done = bf16[16384,349]{1,0:T(8,128)(2,1)} async-done(((bf16[2048,349]{1,0:T(8,128)(2,1)}), bf16[16384,349]{1,0:T(8,128)(2,1)}) %all-gather.5.cloned.1.call-update) | async-done | bytes 11436048 | tf_op jit(solution)/shard_map/all_gather | solution.py:23
  158.9 36.0 %fusion.24 = (f32[2048]{0:T(1024)S(1)}, f32[349,2048]{1,0:T(8,128)}) fusion(bf16[16384,349]{1,0:T(8,128)(2,1)} %all-gather.5.cloned.1.call-done, bf16[2048,16384]{1,0:T(8,128)(2,1)} %param.6), kind=kOutput, calls=%fused_computation.37 | convolution fusion | flops 23421706240 | bytes 81412096 | tf_op jit(solution)/shard_map/dot_general | solution.py:24
  194.9 0.0 copy-start.2
  194.9 0.0 copy-done.3
  194.9 2.5 fusion.2
  197.5 0.0 copy-done.2
  197.5 0.6 convert_reduce_fusion
  198.1 22.7 %all-reduce = (f32[]{:T(128)}, f32[]{:T(128)}) all-reduce(f32[]{:T(128)} %get-tuple-element.9, f32[]{:T(128)} %get-tuple-element.8), channel_id=1, replica_groups=mesh['nodes'=8] {'nodes'}, use_global_device_ids=true, to_apply=%region_4.0 | all-reduce | flops 2 | bytes 16 | tf_op jit(solution)/shard_map/psum | solution.py:30
  220.8 0.6 convert_divide_fusion
  221.4 37.1 %convolution_bitcast_fusion = f32[16384,349]{0,1:T(8,128)} fusion(bf16[2048,16384]{1,0:T(8,128)(2,1)} %param.6, f32[349,2048]{1,0:T(8,128)} %get-tuple-element.16, f32[2048]{0:T(1024)S(1)} %convert_divide_fusion, f32[2048]{0:T(1024)S(1)} %get-tuple-element.14, s32[2048]{0:T(1024)S(1)} %copy-done.3), kind=kOutput, calls=%fused_computation | convolution fusion | flops 23425282048 | bytes 92864512 | tf_op jit(solution)/shard_map/dot_general | solution.py:8
  258.5 0.0 reduce-scatter.3.cloned.1.call-update
  258.6 0.0 reduce-scatter.5.cloned.1.call-start
  258.6 138.7 %reduce-scatter.3.cloned.1.call-done = f32[2048,349]{0,1:T(8,128)} async-done(((f32[16384,349]{0,1:T(8,128)}), f32[2048,349]{0,1:T(8,128)}) %reduce-scatter.3.cloned.1.call-update) | async-done | bytes 2859024 | tf_op jit(solution)/shard_map/reduce_scatter | solution.py:34
  397.3 32.7 %convolution_bitcast_fusion.1 = f32[16384,256]{0,1:T(8,128)} fusion(bf16[2048,16384]{1,0:T(8,128)(2,1)} %param.6, f32[256,2048]{1,0:T(8,128)S(1)} %fusion.25, f32[2048,349]{0,1:T(8,128)} %reduce-scatter.3.cloned.1.call-done, f32[256,349]{0,1:T(8,128)S(1)} %copy-done.1), kind=kOutput, calls=%fused_computation.1 | convolution fusion | flops 17548199936 | bytes 89199616 | tf_op jit(solution)/shard_map/dot_general | solution.py:8
  430.0 0.0 reduce-scatter.5.cloned.1.call-update
  430.0 0.0 all-reduce.4.cloned.1.call-start
  430.1 3.1 fusion.13
  433.2 103.9 %reduce-scatter.5.cloned.1.call-done = f32[2048,256]{0,1:T(8,128)} async-done(((f32[16384,256]{0,1:T(8,128)}), f32[2048,256]{0,1:T(8,128)}) %reduce-scatter.5.cloned.1.call-update) | async-done | bytes 2097168 | tf_op jit(solution)/shard_map/reduce_scatter | solution.py:39
  537.1 2.7 convolution_bitcast_fusion.2
  539.8 0.0 all-reduce.4.cloned.1.call-update
  541.1 43.0 %all-reduce.4.cloned.1.call-done = (f32[128,256]{0,1:T(8,128)}, f32[256,349]{0,1:T(8,128)}) async-done(((f32[128,256]{0,1:T(8,128)}, f32[256,349]{0,1:T(8,128)}), (f32[128,256]{0,1:T(8,128)}, f32[256,349]{0,1:T(8,128)})) %all-reduce.4.cloned.1.call-update) | async-done | bytes 488464 | tf_op jit(solution)/shard_map/psum | solution.py:40
  584.1 1.7 copy.9
  585.8 1.7 copy.12
  (1 shorter events, 0.0 us)
Async XLA Ops:
  7.2 1.0 copy-start
  7.2 54.8 %all-gather.3.cloned.1.call-start = ((), (), s32[]{:S(2)}) async-start(), calls=%async_computation.2 | async-start | bytes 9437184 | tf_op jit(solution)/shard_map/all_gather | solution.py:19
  10.6 79.8 %copy-start.1 = (f32[256,349]{0,1:T(8,128)S(1)}, f32[256,349]{0,1:T(8,128)}, u32[]{:S(2)}) copy-start(f32[256,349]{0,1:T(8,128)} %param.9) | copy-start | bytes 1072132
  10.6 148.3 %all-gather.5.cloned.1.call-start = ((), (), s32[]{:S(2)}) async-start(), calls=%async_computation.3 | async-start | bytes 14155776 | tf_op jit(solution)/shard_map/all_gather | solution.py:23
  92.5 102.5 %copy-start.3 = (s32[2048]{0:T(1024)S(1)}, s32[2048]{0:T(1024)}, u32[]{:S(2)}) copy-start(s32[2048]{0:T(1024)} %param.10) | copy-start | bytes 24580
  92.5 304.8 %reduce-scatter.3.cloned.1.call-start = ((), (), s32[]{:S(2)}) async-start(), calls=%async_computation.4 | async-start | bytes 25952256 | tf_op jit(solution)/shard_map/reduce_scatter | solution.py:34
  194.9 2.6 copy-start.2
  258.6 278.5 %reduce-scatter.5.cloned.1.call-start = ((), (), s32[]{:S(2)}) async-start(), calls=%async_computation.5 | async-start | bytes 18874368 | tf_op jit(solution)/shard_map/reduce_scatter | solution.py:39
  430.0 154.1 %all-reduce.4.cloned.1.call-start = ((), (), s32[]{:S(2)}) async-start(), calls=%async_computation.6 | async-start | bytes 983040 | tf_op jit(solution)/shard_map/psum | solution.py:40
Sparse Core Ops, SparseCore 0:
  10.8 51.1 all-gather.2
  92.6 66.2 all-gather.4
  258.7 138.5 reduce-scatter.2
  430.1 106.9 reduce-scatter.4
  540.7 43.3 all-reduce.3
where the time goes:
time: 596 us; the launch traced here: 595 us
  waiting for transfers between devices  403 us (68%)
  matrix products  144 us (24%)
  blocking collectives  22.7 us (4%)
  between operations  16.3 us (3%)
    reduce_scatter x1, waiting for transfers between devices, local_step(): lax.psum_scatter(part_y2, node_axis, scatter_dimension=0, tiled=True)  139 us
    reduce_scatter x1, waiting for transfers between devices, local_step(): lax.psum_scatter(part_y1, node_axis, scatter_dimension=0, tiled=True)  104 us
    dot_general x4, matrix products, contract_rows(): lax.dot_general(left, right, (((0,), (0,)), ((), ())), preferred_element_...  75.6 us
    all_gather x1, waiting for transfers between devices, local_step(): y_two_all = lax.all_gather(y_two, node_axis, tiled=True)  66.4 us
    all_gather x1, waiting for transfers between devices, local_step(): y_one_all = lax.all_gather(y_one, node_axis, tiled=True)  51.3 us
    psum x1, waiting for transfers between devices, local_step(): grad_one = lax.psum(contract_rows(feat_rows, grad_y1), node_axis)  43 us
    dot_general x1, matrix products, local_step(): z_two = jnp.dot(adj_rows, y_two_all, preferred_element_type=jnp.float32)  36 us
    dot_general x1, matrix products, local_step(): z_one = jnp.dot(adj_rows, y_one_all, preferred_element_type=jnp.float32)  28.5 us
  transfers between devices with their start and end apart: 5, of which 5 were waited for; matrix products, arithmetic and copies ran while one was open for 1% of the time, Pallas kernels for 0%

commit v1 on v0

v1 whole, which is shorter than its diff:
```python
import jax
import jax.numpy as jnp
from jax import lax
from jax.sharding import PartitionSpec as P


def contract_rows(left, right):
    return lax.dot_general(left, right, (((0,), (0,)), ((), ())), preferred_element_type=jnp.float32)


def mm(left, right):
    return jnp.dot(left, right, preferred_element_type=jnp.float32)


def solution(mesh):
    node_axis = mesh.axis_names[0]

    def gather(x):
        return lax.all_gather(x, node_axis, tiled=True)

    def local_step(adj_rows, feat_rows, w_one, w_two, label_rows, mask_rows):
        classes = w_two.shape[1]
        w_one_b = w_one.astype(jnp.bfloat16)
        w_two_b = w_two.astype(jnp.bfloat16)
        y_one_all = mm(gather(feat_rows), w_one_b).astype(jnp.bfloat16)
        z_one = mm(adj_rows, y_one_all)
        h_one = jnp.maximum(z_one, 0.0).astype(jnp.bfloat16)
        y_two_all = mm(gather(h_one), w_two_b).astype(jnp.bfloat16)
        z_two = mm(adj_rows, y_two_all)
        mask_f = mask_rows.astype(jnp.float32)
        label_count = lax.psum(jnp.sum(mask_f), node_axis)
        log_norm = jax.nn.logsumexp(z_two, axis=1)
        onehot = (label_rows[:, None] == jnp.arange(classes, dtype=jnp.int32)[None, :]).astype(jnp.float32)
        picked = jnp.sum(z_two * onehot, axis=1)
        loss_part = jnp.sum(mask_f * (log_norm - picked))
        soft_probs = jnp.exp(z_two - log_norm[:, None])
        g_two = ((soft_probs - onehot) * (mask_f / label_count)[:, None]).astype(jnp.bfloat16)
        grad_y2 = mm(adj_rows, gather(g_two)).astype(jnp.bfloat16)
        grad_h1 = lax.dot_general(grad_y2, w_two_b, (((1,), (1,)), ((), ())), preferred_element_type=jnp.float32)
        grad_z1 = jnp.where(z_one > 0.0, grad_h1, 0.0).astype(jnp.bfloat16)
        grad_y1 = mm(adj_rows, gather(grad_z1)).astype(jnp.bfloat16)
        loss_sum, grad_one, grad_two = lax.psum(
            (loss_part, contract_rows(feat_rows, grad_y1), contract_rows(h_one, grad_y2)), node_axis)
        return loss_sum / label_count, grad_one, grad_two

    return jax.shard_map(local_step, mesh=mesh, in_specs=(P(node_axis, None), P(node_axis, None), P(None, None), P(None, None), P(node_axis), P(node_axis)), out_specs=(P(), P(None, None), P(None, None)), check_vma=False)
```

time: 596 us -> 433 us (0.73)
  waiting for transfers between devices: 403 us -> 238 us
    reduce_scatter x2 -> x0, waiting for transfers between devices: 243 us -> none  [the longest x1 139 us: local_step(): lax.psum_scatter(part_y2, node_axis, scatter_dimension=0, tiled=True)]
    all_gather x2 -> x4, waiting for transfers between devices: 118 us -> 195 us  [gather(): return lax.all_gather(x, node_axis, tiled=True)]
    dot_general x4 -> x2, matrix products: 75.6 us -> 2.39 us  [contract_rows(): lax.dot_general(left, right, (((0,), (0,)), ((), ())), preferred_element_...]
    dot_general x4 -> x7, matrix products: 68.9 us -> 141 us  [the longest x6 138 us: mm(): return jnp.dot(left, right, preferred_element_type=jnp.float32)]
  transfers between devices with their start and end apart: 5 -> 5, of which waited for: 5 -> 5; matrix products, arithmetic and copies ran while one was open for 1% -> 0% of each run, Pallas kernels for 0% -> 0%
where the time goes in v1:
time: 433 us
  waiting for transfers between devices  238 us (55%)
  matrix products  144 us (33%)
  blocking collectives  22.7 us (5%)
  between operations  16.2 us (4%)
  other arithmetic  8.67 us (2%)
    all_gather x4, waiting for transfers between devices, gather(): return lax.all_gather(x, node_axis, tiled=True)  195 us
    dot_general x6, matrix products, mm(): return jnp.dot(left, right, preferred_element_type=jnp.float32)  138 us
    psum x1, waiting for transfers between devices, local_step(): lax.psum((loss_part, contract_rows(feat_rows, grad_y1), contract_rows(h_o...  42.2 us
    psum x1, blocking collectives, local_step(): lax.psum((loss_part, contract_rows(feat_rows, grad_y1), contract_rows(h_o...  22.7 us
  transfers between devices with their start and end apart: 5, of which 5 were waited for; matrix products, arithmetic and copies ran while one was open for 0% of the time, Pallas kernels for 0%

profile of v1, /device:TPU:0, one launch (start us, length us, event | category | flops | bytes accessed | tf_op | source)
XLA Modules:
  0.0 432.6 jit_solution(9296106446437581024)
XLA Ops:
  7.2 0.0 all-gather.5.cloned.1.call-start
  7.2 0.7 all-gather.5.cloned.1.call-update
  7.9 0.0 all-gather.7.cloned.1.call-start
  7.9 35.5 %all-gather.5.cloned.1.call-done = bf16[16384,128]{1,0:T(8,128)(2,1)} async-done(((bf16[2048,128]{1,0:T(8,128)(2,1)}), bf16[16384,128]{1,0:T(8,128)(2,1)}) %all-gather.5.cloned.1.call-update) | async-done | bytes 4194320 | tf_op jit(solution)/shard_map/all_gather | solution.py:19
  43.4 7.7 %convolution_convert_fusion.1.clone.4 = bf16[16384,256]{1,0:T(8,128)(2,1)} fusion(bf16[16384,128]{1,0:T(8,128)(2,1)} %all-gather.5.cloned.1.call-done, f32[128,256]{1,0:T(8,128)} %param.8), kind=kOutput, calls=%fused_computation.1.clone.clone.clone.1 | convolution fusion | flops 1077968896 | bytes 12713984 | tf_op jit(solution)/shard_map/dot_general | solution.py:12
  51.1 28.5 %fusion.8 = f32[256,2048]{1,0:T(8,128)S(1)} fusion(bf16[2048,16384]{1,0:T(8,128)(2,1)} %param.6, bf16[16384,256]{1,0:T(8,128)(2,1)} %convolution_convert_fusion.1.clone.4), kind=kOutput, calls=%fused_computation.14 | convolution fusion | flops 17179869184 | bytes 77594624 | tf_op jit(solution)/shard_map/dot_general | solution.py:12
  79.7 0.0 copy-start.1
  79.7 1.1 fusion.11
  80.8 0.0 all-gather.7.cloned.1.call-update
  80.8 0.0 all-gather.9.cloned.1.call-start
  80.9 48.4 %all-gather.7.cloned.1.call-done = bf16[16384,256]{0,1:T(8,128)(2,1)} async-done(((bf16[2048,256]{0,1:T(8,128)(2,1)}), bf16[16384,256]{0,1:T(8,128)(2,1)}) %all-gather.7.cloned.1.call-update) | async-done | bytes 8388624 | tf_op jit(solution)/shard_map/all_gather | solution.py:19
  129.3 0.0 copy-done.1
  129.3 9.4 %convolution_convert_fusion.clone.1.clone.4 = bf16[16384,349]{0,1:T(8,128)(2,1)} fusion(bf16[16384,256]{0,1:T(8,128)(2,1)} %all-gather.7.cloned.1.call-done, f32[256,349]{0,1:T(8,128)S(1)} %copy-done.1), kind=kOutput, calls=%fused_computation.clone.clone.clone.clone.clone.1 | convolution fusion | flops 2933431552 | bytes 20182016 | tf_op jit(solution)/shard_map/dot_general | solution.py:12
  138.7 0.0 copy-start.2
  138.7 33.3 %fusion.18 = (f32[2048]{0:T(1024)S(1)}, f32[349,2048]{1,0:T(8,128)}) fusion(bf16[2048,16384]{1,0:T(8,128)(2,1)} %param.6, bf16[16384,349]{0,1:T(8,128)(2,1)} %convolution_convert_fusion.clone.1.clone.4), kind=kOutput, calls=%fused_computation.32 | convolution fusion | flops 23421706240 | bytes 81412096 | tf_op jit(solution)/shard_map/dot_general | solution.py:12
  172.0 0.0 copy-start.3
  172.0 0.0 copy-done.2
  172.0 2.5 fusion.3
  174.6 0.0 copy-done.3
  174.6 0.6 convert_reduce_fusion
  175.2 22.7 %all-reduce = (f32[]{:T(128)}, f32[]{:T(128)}) all-reduce(f32[]{:T(128)} %get-tuple-element.12, f32[]{:T(128)} %get-tuple-element.11), channel_id=1, replica_groups=mesh['nodes'=8] {'nodes'}, use_global_device_ids=true, to_apply=%region_4.0 | all-reduce | flops 2 | bytes 16 | tf_op jit(solution)/shard_map/psum | solution.py:42
  197.9 0.6 convert_divide_fusion
  198.5 3.7 fusion.7
  202.2 0.0 all-gather.9.cloned.1.call-update
  202.3 0.0 all-gather.11.cloned.1.call-start
  202.3 63.9 %all-gather.9.cloned.1.call-done = bf16[16384,349]{0,1:T(8,128)(2,1)} async-done(((bf16[2048,349]{0,1:T(8,128)(2,1)}), bf16[16384,349]{0,1:T(8,128)(2,1)}) %all-gather.9.cloned.1.call-update) | async-done | bytes 11436048 | tf_op jit(solution)/shard_map/all_gather | solution.py:19
  266.2 32.0 %convolution_convert_fusion.2 = bf16[349,2048]{1,0:T(8,128)(2,1)S(1)} fusion(bf16[16384,349]{0,1:T(8,128)(2,1)} %all-gather.9.cloned.1.call-done, bf16[2048,16384]{1,0:T(8,128)(2,1)} %param.6), kind=kOutput, calls=%fused_computation.15 | convolution fusion | flops 23421708288 | bytes 79974400 | tf_op jit(solution)/shard_map/dot_general | solution.py:12
  298.2 2.8 fusion.9
  300.9 0.0 all-gather.11.cloned.1.call-update
  301.0 0.0 all-reduce.4.cloned.1.call-start
  301.0 1.3 fusion.10
  302.3 0.0 copy-start
  302.3 47.1 %all-gather.11.cloned.1.call-done = bf16[16384,256]{0,1:T(8,128)(2,1)} async-done(((bf16[2048,256]{0,1:T(8,128)(2,1)}), bf16[16384,256]{0,1:T(8,128)(2,1)}) %all-gather.11.cloned.1.call-update) | async-done | bytes 8388624 | tf_op jit(solution)/shard_map/all_gather | solution.py:19
  349.5 27.4 %convolution_convert_fusion.3 = bf16[256,2048]{1,0:T(8,128)(2,1)S(1)} fusion(bf16[16384,256]{0,1:T(8,128)(2,1)} %all-gather.11.cloned.1.call-done, bf16[2048,16384]{1,0:T(8,128)(2,1)} %param.6), kind=kOutput, calls=%fused_computation.18 | convolution fusion | flops 17180393472 | bytes 76546048 | tf_op jit(solution)/shard_map/dot_general | solution.py:12
  376.9 0.0 copy-done
  376.9 1.1 convolution_bitcast_fusion
  378.0 0.0 all-reduce.4.cloned.1.call-update
  379.2 42.2 %all-reduce.4.cloned.1.call-done = (f32[128,256]{0,1:T(8,128)}, f32[256,349]{0,1:T(8,128)}) async-done(((f32[128,256]{0,1:T(8,128)}, f32[256,349]{0,1:T(8,128)}), (f32[128,256]{0,1:T(8,128)}, f32[256,349]{0,1:T(8,128)})) %all-reduce.4.cloned.1.call-update) | async-done | bytes 488464 | tf_op jit(solution)/shard_map/psum | solution.py:42
  421.5 1.7 copy.10
  423.1 1.7 copy.13
  (1 shorter events, 0.0 us)
Async XLA Ops:
  7.2 36.2 %all-gather.5.cloned.1.call-start = ((), (), s32[]{:S(2)}) async-start(), calls=%async_computation | async-start | bytes 4718592 | tf_op jit(solution)/shard_map/all_gather | solution.py:19
  7.9 121.4 %all-gather.7.cloned.1.call-start = ((), (), s32[]{:S(2)}) async-start(), calls=%async_computation.1 | async-start | bytes 9437184 | tf_op jit(solution)/shard_map/all_gather | solution.py:19
  79.7 49.7 %copy-start.1 = (f32[256,349]{0,1:T(8,128)S(1)}, f32[256,349]{0,1:T(8,128)}, u32[]{:S(2)}) copy-start(f32[256,349]{0,1:T(8,128)} %param.9) | copy-start | bytes 1072132
  80.8 185.3 %all-gather.9.cloned.1.call-start = ((), (), s32[]{:S(2)}) async-start(), calls=%async_computation.2 | async-start | bytes 12976128 | tf_op jit(solution)/shard_map/all_gather | solution.py:19
  138.7 33.3 %copy-start.2 = (s32[2048]{0:T(1024)S(1)}, s32[2048]{0:T(1024)}, u32[]{:S(2)}) copy-start(s32[2048]{0:T(1024)} %param.10) | copy-start | bytes 24580
  172.0 2.6 copy-start.3
  202.3 147.2 %all-gather.11.cloned.1.call-start = ((), (), s32[]{:S(2)}) async-start(), calls=%async_computation.3 | async-start | bytes 9437184 | tf_op jit(solution)/shard_map/all_gather | solution.py:19
  301.0 120.5 %all-reduce.4.cloned.1.call-start = ((), (), s32[]{:S(2)}) async-start(), calls=%async_computation.4 | async-start | bytes 983040 | tf_op jit(solution)/shard_map/psum | solution.py:42
  302.3 74.5 %copy-start = (bf16[2048,128]{1,0:T(8,128)(2,1)S(1)}, bf16[2048,128]{1,0:T(8,128)(2,1)}, u32[]{:S(2)}) copy-start(bf16[2048,128]{1,0:T(8,128)(2,1)} %param.7) | copy-start | bytes 1572868
Sparse Core Ops, SparseCore 0:
  9.8 33.5 all-gather.4
  81.0 48.3 all-gather.6
  202.4 63.7 all-gather.8
  301.1 48.3 all-gather.10
  378.1 43.3 all-reduce.3

commit v2 on v1

v2 whole, which is shorter than its diff:
```python
import functools

import jax
import jax.numpy as jnp
from jax import lax
from jax.experimental import pallas as pl
from jax.experimental.pallas import tpu as pltpu
from jax.sharding import PartitionSpec as P

MESH = pl.DeviceIdType.MESH
F32, BF16 = jnp.float32, jnp.bfloat16
SLOTS = 4
CHUNK = 512
CHUNKS = 4
ITEMS = 16
LANES = 128


def nt(left, right):
    return lax.dot_general(left, right, (((1,), (1,)), ((), ())), preferred_element_type=F32)


def nn(left, right):
    return jnp.dot(left, right, preferred_element_type=F32)


def gcn_kernel(axis, classes, a_hbm, x_hbm, w1_ref, w2_ref, lab_ref, mask_ref, loss_ref, dw1_ref, dw2_ref,
               ring, xg, hg, gg, dg, acc1, acc2, lhs, e2, w1t, w2t, w2b, cnt, los, mrow,
               s1, s2, ta1, ta2, tc1, tc2, hb1, hb2, tb1, tb2,
               a_sem, x_sem, isend, irecv, dsend, drecv, csend, crecv, lsend, lrecv, rsend, rrecv):
    me = lax.axis_index(axis)
    core, chip = lax.rem(me, 2), lax.div(me, 2)
    cx, cy = lax.rem(chip, 2), lax.div(chip, 2)
    hidden = hg.shape[2]
    rows_p = gg.shape[2]

    def chip_of(m):
        return lax.rem(cy + m // 2, 2) * 2 + lax.rem(cx + m % 2, 2)

    def chip_dyn(m):
        return lax.rem(cy + lax.div(m, 2), 2) * 2 + lax.rem(cx + lax.rem(m, 2), 2)

    partner = chip * 2 + (1 - core)
    to_x, to_y, to_d = (chip_of(m) * 2 + core for m in (1, 2, 3))
    bufs = (xg, hg, gg, dg)

    def rcopy(src, dst, send, recv, dev):
        return pltpu.make_async_remote_copy(src_ref=src, dst_ref=dst, send_sem=send, recv_sem=recv,
                                            device_id=(dev,), device_id_type=MESH)

    def a_copies(i, slot):
        first = chip_dyn(lax.div(i, 4)) * (2 * CHUNK * CHUNKS) + lax.rem(i, 4) * CHUNK
        for h in (0, 1):
            cols = pl.ds(pl.multiple_of(first + h * CHUNK * CHUNKS, CHUNK), CHUNK)
            yield pltpu.make_async_copy(a_hbm.at[:, cols], ring.at[slot, h], a_sem.at[slot, h])

    def own_copies(p, j):
        g, q = bufs[p].at[me, j], p % 2
        return [rcopy(g, g, isend.at[q, 0, j], irecv.at[q, 0, j], to_x),
                rcopy(g, g, isend.at[q, 1, j], irecv.at[q, 1, j], to_y),
                rcopy(g, g, dsend.at[q, 0, j], drecv.at[q, 0, j], partner)]

    def relay_x(p, j):
        g, q, half = bufs[p], p % 2, bufs[p].shape[2] // 2
        g = g.at[to_y, j, pl.ds(0, half)]
        return rcopy(g, g, isend.at[q, 2, j], irecv.at[q, 2, j], to_x)

    def relay_y(p, j):
        g, q, half = bufs[p], p % 2, bufs[p].shape[2] // 2
        g = g.at[to_x, j, pl.ds(half, half)]
        return rcopy(g, g, isend.at[q, 3, j], irecv.at[q, 3, j], to_y)

    def forward(p, m, j):
        g, q = bufs[p].at[chip_of(m) * 2 + core, j], p % 2
        return rcopy(g, g, dsend.at[q, m, j], drecv.at[q, m, j], partner)

    def arrive_xy(p, j):
        q = p % 2
        g = bufs[p].at[to_x, j]
        rcopy(g, g, isend.at[q, 0, j], irecv.at[q, 0, j], to_x).wait_recv()
        relay_y(p, j).start()
        forward(p, 1, j).start()
        g = bufs[p].at[to_y, j]
        rcopy(g, g, isend.at[q, 1, j], irecv.at[q, 1, j], to_y).wait_recv()
        relay_x(p, j).start()
        forward(p, 2, j).start()

    def arrive_d(p, j):
        q, half = p % 2, bufs[p].shape[2] // 2
        g = bufs[p].at[to_d, j, pl.ds(0, half)]
        rcopy(g, g, isend.at[q, 2, j], irecv.at[q, 2, j], to_x).wait_recv()
        g = bufs[p].at[to_d, j, pl.ds(half, half)]
        rcopy(g, g, isend.at[q, 3, j], irecv.at[q, 3, j], to_y).wait_recv()
        forward(p, 3, j).start()

    def arrive_core(p, m, j):
        q = p % 2
        g = bufs[p].at[chip_dyn(m) * 2 + 1 - core, j]
        rcopy(g, g, dsend.at[q, m, j], drecv.at[q, m, j], partner).wait_recv()

    def wait_sends(p, j):
        for copy in own_copies(p, j) + [relay_x(p, j), relay_y(p, j)] + [forward(p, m, j) for m in (1, 2, 3)]:
            copy.wait_send()

    def tile_copies(buf, send, recv):
        for k in range(1, 8):
            yield rcopy(buf.at[me], buf.at[me], send.at[k - 1], recv.at[k - 1], lax.rem(me + k, 8))

    def wait_tiles(buf, send, recv):
        for k, copy in enumerate(tile_copies(buf, send, recv), 1):
            copy.wait_send()
            other = lax.rem(me + 8 - k, 8)
            rcopy(buf.at[other], buf.at[other], send.at[k - 1], recv.at[k - 1], other).wait_recv()

    class Reduce:
        def __init__(self, src, ta, tc, hb, tb, n):
            self.src, self.ta, self.tc, self.hb, self.tb, self.n = src, ta, tc, hb, tb, n
            self.a = rcopy(src.at[1 - core], ta, rsend.at[n, 0], rrecv.at[n, 0], partner)
            self.b1 = [rcopy(hb.at[chip_of(m)], tb.at[m - 1], rsend.at[n, m], rrecv.at[n, m], chip_of(m) * 2 + core)
                       for m in (1, 2, 3)]
            self.b2 = [rcopy(src.at[core, chip], src.at[core, chip], rsend.at[n, 3 + m], rrecv.at[n, 3 + m],
                             chip_of(m) * 2 + core) for m in (1, 2, 3)]
            self.c = rcopy(src.at[core], tc, rsend.at[n, 7], rrecv.at[n, 7], partner)

        def first(self):
            self.a.start()

        def second(self):
            self.a.wait()
            self.hb[...] = self.src[core] + self.ta[...]
            for copy in self.b1:
                copy.start()

        def third(self):
            for copy in self.b1:
                copy.wait()
            self.src[core, chip] = self.hb[chip] + self.tb[0] + self.tb[1] + self.tb[2]
            for copy in self.b2:
                copy.start()

        def fourth(self):
            for m, copy in enumerate(self.b2, 1):
                copy.wait_send()
                g = self.src.at[core, chip_of(m)]
                rcopy(g, g, rsend.at[self.n, 3 + m], rrecv.at[self.n, 3 + m], chip_of(m) * 2 + core).wait_recv()
            self.c.start()

        def last(self, out):
            self.c.wait()
            for k in range(4):
                out[pl.ds(pl.multiple_of(core * 128 + k * 32, 32), 32), :] = self.src[core, k]
                out[pl.ds(pl.multiple_of((1 - core) * 128 + k * 32, 32), 32), :] = self.tc[k]

    reduce1, reduce2 = Reduce(s1, ta1, tc1, hb1, tb1, 0), Reduce(s2, ta2, tc2, hb2, tb2, 1)

    x_copies = [pltpu.make_async_copy(x_hbm.at[j], xg.at[me, j], x_sem.at[j]) for j in range(CHUNKS)]
    for copy in x_copies:
        copy.start()
    for s in range(SLOTS):
        for copy in a_copies(jnp.int32(s), s):
            copy.start()
    cnt[...] = jnp.zeros_like(cnt)
    los[...] = jnp.zeros_like(los)
    cnt[me, 0:1, :] = jnp.sum(mask_ref[...].astype(F32), axis=0)
    barrier = pltpu.get_barrier_semaphore()
    for k in range(1, 8):
        pl.semaphore_signal(barrier, inc=1, device_id=(lax.rem(me + k, 8),), device_id_type=MESH)
    pl.semaphore_wait(barrier, 7)
    for j, copy in enumerate(x_copies):
        copy.wait()
        for send in own_copies(0, j):
            send.start()

    w1t[...] = w1_ref[...].T.astype(BF16)
    w2b[...] = jnp.zeros_like(w2b)
    w2b[:, :classes] = w2_ref[...].astype(BF16)
    w2t[...] = w2b[...].astype(F32).T[:rows_p].astype(BF16)
    e2[:, rows_p:, :] = jnp.zeros((CHUNKS, e2.shape[1] - rows_p, CHUNK), BF16)
    for copy in tile_copies(cnt, csend, crecv):
        copy.start()

    def operands(p, m, j):
        refs = []
        for h in (0, 1):
            dev = chip_dyn(m) * 2 + h
            if p == 0:
                lhs[h, :hidden, :] = nt(w1t[...], xg[dev, j]).astype(BF16)
                refs.append(lhs.at[h, pl.ds(0, hidden)])
            elif p == 1:
                lhs[h] = nn(w2t[...], hg[dev, j]).astype(BF16)
                refs.append(lhs.at[h])
            else:
                refs.append(bufs[p].at[dev, j])
        return refs

    def product(refs, slot, rc):
        rows = pl.ds(rc * CHUNK, CHUNK) if isinstance(rc, int) else pl.ds(pl.multiple_of(rc * CHUNK, CHUNK), CHUNK)
        return nt(refs[0][...], ring[slot, 0, rows, :]) + nt(refs[1][...], ring[slot, 1, rows, :])

    def finish_one(rc):
        z = acc1[rc]
        hg[me, rc] = jnp.maximum(z, 0.0).astype(BF16)

    def finish_two(rc):
        for b in range(CHUNK // LANES):
            lanes = pl.ds(b * LANES, LANES)
            z = acc2[rc, :, lanes]
            index = lax.broadcasted_iota(jnp.int32, z.shape, 0)
            z = jnp.where(index < classes, z, -jnp.inf)
            top = jnp.max(z, axis=0, keepdims=True)
            e = jnp.exp(z - top)
            total = jnp.sum(e, axis=0, keepdims=True)
            hit = index == lab_ref[rc, :, lanes]
            picked = jnp.sum(jnp.where(hit, z, 0.0), axis=0, keepdims=True)
            mask_f = mask_ref[rc, :, lanes].astype(F32)
            los[me, 0:1, lanes] += mask_f * (jnp.log(total) + top - picked)
            onehot = jnp.where(hit, 1.0, 0.0)
            gg[me, rc, :, lanes] = ((e * (1.0 / total) - onehot) * (mask_f / mrow[:, lanes])).astype(BF16)

    def finish_three(rc):
        e2[rc, :rows_p, :] = acc2[rc].astype(BF16)
        dz = nn(w2b[...], e2[rc])
        dg[me, rc] = jnp.where(acc1[rc] > 0.0, dz, 0.0).astype(BF16)

    def finish_four(rc):
        return nn(acc1[rc].astype(BF16), xg[me, rc])

    def phase(p):
        acc = (acc1, acc2, acc2, acc1)[p]

        if p == 1:
            wait_tiles(cnt, csend, crecv)
            total = jnp.sum(jnp.sum(cnt[...], axis=0), axis=0, keepdims=True)
            mrow[...] = jnp.broadcast_to(jnp.sum(total, axis=1, keepdims=True), mrow.shape)
        if p == 3:
            grad = nt(hg[me, 0], e2[0])
            for rc in range(1, CHUNKS):
                grad = grad + nt(hg[me, rc], e2[rc])
            for k in range(8):
                s2[k // 4, k % 4] = grad[k * 32:(k + 1) * 32]
        acc[...] = jnp.zeros_like(acc)
        if p == 2:
            for copy in tile_copies(los, lsend, lrecv):
                copy.start()
        if p == 3:
            reduce2.first()

        def step(i, carry):
            m, j = lax.div(i, 4), lax.rem(i, 4)
            slot = lax.rem(i + p * ITEMS, SLOTS)

            @pl.when((i >= 3) & (i <= 6))
            def _():
                arrive_xy(p, i - 3)

            @pl.when(i >= 11)
            def _():
                arrive_d(p, i - 11)

            if p > 0:
                @pl.when(i < 4)
                def _():
                    wait_sends(p - 1, i)

            if p == 3:
                for at, stage in ((1, reduce2.second), (4, reduce2.third), (7, reduce2.fourth)):
                    pl.when(i == at)(stage)

            arrive_core(p, m, j)
            for copy in a_copies(i, slot):
                copy.wait()
            refs = operands(p, m, j)
            for rc in range(CHUNKS):
                acc[rc] += product(refs, slot, rc)

            def prefetch():
                for copy in a_copies(lax.rem(i + SLOTS, ITEMS), slot):
                    copy.start()

            if p < 3:
                prefetch()
            else:
                pl.when(i + SLOTS < ITEMS)(prefetch)
            return carry

        lax.fori_loop(0, ITEMS - 1, step, 0)

        i = jnp.int32(ITEMS - 1)
        slot = (ITEMS - 1 + p * ITEMS) % SLOTS
        arrive_core(p, jnp.int32(3), CHUNKS - 1)
        for copy in a_copies(i, slot):
            copy.wait()
        refs = operands(p, jnp.int32(3), CHUNKS - 1)

        def finish(rc, carry):
            acc[rc] += product(refs, slot, rc)
            if p < 3:
                (finish_one, finish_two, finish_three)[p](rc)
                for copy in own_copies(p + 1, rc):
                    copy.start()
                return carry
            return carry + finish_four(rc)

        out = lax.fori_loop(0, CHUNKS, finish, jnp.zeros((hidden, LANES), F32) if p == 3 else 0)
        if p < 3:
            for copy in a_copies(jnp.int32((ITEMS - 1 + SLOTS) % ITEMS), slot):
                copy.start()
        return out

    for p in range(4):
        out = phase(p)

    for k in range(8):
        s1[k // 4, k % 4] = out[k * 32:(k + 1) * 32]
    reduce1.first()
    reduce2.last(dw2_ref)
    wait_tiles(los, lsend, lrecv)
    total = jnp.sum(jnp.sum(los[...], axis=0), axis=0, keepdims=True)
    total = jnp.sum(total, axis=1, keepdims=True) / mrow[:, 0:1]
    loss_ref[...] = jnp.broadcast_to(total, loss_ref.shape)
    reduce1.second()
    for j in range(CHUNKS):
        wait_sends(3, j)
    reduce1.third()
    reduce1.fourth()
    reduce1.last(dw1_ref)


def solution(mesh):
    axis = mesh.axis_names[0]

    def local_step(adj_rows, feat_rows, w_one, w_two, label_rows, mask_rows):
        f_in, hidden = w_one.shape
        classes = w_two.shape[1]
        rows_p = -(-classes // 32) * 32
        lanes_p = -(-classes // LANES) * LANES
        rows = adj_rows.shape[0]
        dma = pltpu.SemaphoreType.DMA
        vmem = pl.BlockSpec(memory_space=pltpu.VMEM)
        hbm = pl.BlockSpec(memory_space=pl.ANY)
        loss, dw1, dw2 = pl.pallas_call(
            functools.partial(gcn_kernel, axis, classes),
            name="gcn_step",
            out_shape=(jax.ShapeDtypeStruct((8, LANES), F32), jax.ShapeDtypeStruct((hidden, f_in), F32),
                       jax.ShapeDtypeStruct((hidden, lanes_p), F32)),
            in_specs=[hbm, hbm, vmem, vmem, vmem, vmem],
            out_specs=(vmem, vmem, vmem),
            scratch_shapes=[
                pltpu.VMEM((SLOTS, 2, rows, CHUNK), BF16),
                pltpu.VMEM((8, CHUNKS, CHUNK, f_in), BF16),
                pltpu.VMEM((8, CHUNKS, hidden, CHUNK), BF16),
                pltpu.VMEM((8, CHUNKS, rows_p, CHUNK), BF16),
                pltpu.VMEM((8, CHUNKS, hidden, CHUNK), BF16),
                pltpu.VMEM((CHUNKS, hidden, CHUNK), F32),
                pltpu.VMEM((CHUNKS, rows_p, CHUNK), F32),
                pltpu.VMEM((2, rows_p, CHUNK), BF16),
                pltpu.VMEM((CHUNKS, lanes_p, CHUNK), BF16),
                pltpu.VMEM((hidden, f_in), BF16),
                pltpu.VMEM((rows_p, hidden), BF16),
                pltpu.VMEM((hidden, lanes_p), BF16),
                pltpu.VMEM((8, 8, CHUNK), F32),
                pltpu.VMEM((8, 8, CHUNK), F32),
                pltpu.VMEM((1, CHUNK), F32),
                pltpu.VMEM((2, 4, 32, f_in), F32),
                pltpu.VMEM((2, 4, 32, lanes_p), F32),
                pltpu.VMEM((4, 32, f_in), F32),
                pltpu.VMEM((4, 32, lanes_p), F32),
                pltpu.VMEM((4, 32, f_in), F32),
                pltpu.VMEM((4, 32, lanes_p), F32),
                pltpu.VMEM((4, 32, f_in), F32),
                pltpu.VMEM((4, 32, lanes_p), F32),
                pltpu.VMEM((3, 32, f_in), F32),
                pltpu.VMEM((3, 32, lanes_p), F32),
                dma((SLOTS, 2)), dma((CHUNKS,)),
                dma((2, 4, CHUNKS)), dma((2, 4, CHUNKS)), dma((2, 4, CHUNKS)), dma((2, 4, CHUNKS)),
                dma((7,)), dma((7,)), dma((7,)), dma((7,)), dma((2, 8)), dma((2, 8)),
            ],
            compiler_params=pltpu.CompilerParams(
                collective_id=0, has_side_effects=True, vmem_limit_bytes=67_000_000),
        )(adj_rows, feat_rows.reshape(CHUNKS, CHUNK, f_in), w_one, w_two,
          label_rows.reshape(CHUNKS, 1, CHUNK), mask_rows.reshape(CHUNKS, 1, CHUNK))
        return loss[0, 0], dw1.T, dw2[:, :classes]

    return jax.shard_map(local_step, mesh=mesh, in_specs=(P(axis, None), P(axis, None), P(None, None), P(None, None), P(axis), P(axis)), out_specs=(P(), P(None, None), P(None, None)), check_vma=False)
```

time: 433 us -> 198 us (0.46)
  waiting for transfers between devices: 238 us -> 0 us
  Pallas kernels: 0 us -> 191 us
  matrix products: 144 us -> 0 us
  blocking collectives: 22.7 us -> 0 us
  between operations: 16.2 us -> 0.64 us
  other arithmetic: 8.67 us -> 0 us
    all_gather x4 -> x0, waiting for transfers between devices: 195 us -> none  [gather(): return lax.all_gather(x, node_axis, tiled=True)]
    pallas_call x0 -> x1, Pallas kernels: none -> 191 us  [local_step(): pl.pallas_call(functools.partial(gcn_kernel, axis, classes), name='gcn_st...]
    dot_general x9 -> x0, matrix products: 144 us -> none  [the longest x6 138 us: mm(): return jnp.dot(left, right, preferred_element_type=jnp.float32)]
    psum x1 -> x0, waiting for transfers between devices: 42.2 us -> none  [local_step(): lax.psum((loss_part, contract_rows(feat_rows, grad_y1), contract_rows(h_o...]
    psum x1 -> x0, blocking collectives: 22.7 us -> none  [local_step(): lax.psum((loss_part, contract_rows(feat_rows, grad_y1), contract_rows(h_o...]
    convert_element_type x2 -> x0, other arithmetic: 4.85 us -> none  [the longest x1 3.71 us: local_step(): ((soft_probs - onehot) * (mask_f / label_count)[:, None]).astype(jnp.bflo...]
  transfers between devices with their start and end apart: 5 -> 0, of which waited for: 5 -> 0; matrix products, arithmetic and copies ran while one was open for 0% -> 0% of each run, Pallas kernels for 0% -> 0%
where the time goes in v2:
time: 198 us
  Pallas kernels  191 us (96%)
  local copies, waits for them, and re-layouts  6.62 us (3%)
    pallas_call x1, Pallas kernels, local_step(): pl.pallas_call(functools.partial(gcn_kernel, axis, classes), name='gcn_st...  191 us
    unnamed x3, local copies, waits for them, and re-layouts  5.43 us

profile of v2, /device:TPU:0, one launch (start us, length us, event | category | flops | bytes accessed | tf_op | source)
XLA Modules:
  0.0 198.1 jit_solution(11212084244202965324)
XLA Ops:
  0.6 1.9 copy.9.w2_ref
  2.5 190.8 %gcn_step.1 = (f32[8,128]{1,0:T(8,128)}, f32[256,128]{1,0:T(8,128)}, f32[256,384]{1,0:T(8,128)}) custom-call(bf16[2048,16384]{1,0:T(8,128)(2,1)} %a_hbm.1, bf16[4,512,128]{2,1,0:T(8,128)(2,1)} %bitcast.6, f32[128,256]{1,0:T(8,128)} %w1_ref.1, f32[256,349]{1,0:T(8,128)} %copy.9.w2_ref, s32[4,1,512]{2,1,0:T(1,128)} %bitcast.9, s32[4,1,512]{2,1,0:T(1,128)} %bitcast.10), custom_call_target="tpu_custom_call" | custom-call | tf_op jit(solution)/shard_map/gcn_step/pallas_call | solution.py:341
  193.3 1.2 slice.6
  194.5 1.7 copy.10
  196.2 1.9 copy.11

commit v3 on v2

v3 whole, which is shorter than its diff:
```python
import functools

import jax
import jax.numpy as jnp
from jax import lax
from jax.experimental import pallas as pl
from jax.experimental.pallas import tpu as pltpu
from jax.sharding import PartitionSpec as P

MESH = pl.DeviceIdType.MESH
F32, BF16 = jnp.float32, jnp.bfloat16
SLOTS = 4
CHUNK = 512
CHUNKS = 4
ITEMS = 16
LANES = 128


def nt(left, right):
    return lax.dot_general(left, right, (((1,), (1,)), ((), ())), preferred_element_type=F32)


def nn(left, right):
    return jnp.dot(left, right, preferred_element_type=F32)


def gcn_kernel(axis, classes, a_hbm, x_hbm, w1_hbm, w2_hbm, lab_hbm, mask_hbm, loss_ref, dw1_ref, dw2_ref,
               ring, xg, hg, gg, dg, acc1, acc2, lhs, e2, xt, w1_ref, w2_ref, lab_ref, mask_ref, w1t, w2t, w2b,
               cnt, los, mrow, d1, r1, f1, s2, ta, tc, hb, tb,
               a_sem, x_sem, w_sem, isend, irecv, dsend, drecv, csend, crecv, lsend, lrecv,
               p1send, p1recv, f1send, f1recv, rsend, rrecv):
    me = lax.axis_index(axis)
    core, chip = lax.rem(me, 2), lax.div(me, 2)
    cx, cy = lax.rem(chip, 2), lax.div(chip, 2)
    hidden = hg.shape[2]
    rows_p = gg.shape[2]

    def chip_of(m):
        return lax.rem(cy + m // 2, 2) * 2 + lax.rem(cx + m % 2, 2)

    def chip_dyn(m):
        return lax.rem(cy + lax.div(m, 2), 2) * 2 + lax.rem(cx + lax.rem(m, 2), 2)

    partner = chip * 2 + (1 - core)
    to_x, to_y, to_d = (chip_of(m) * 2 + core for m in (1, 2, 3))
    bufs = (xg, hg, gg, dg)

    def rcopy(src, dst, send, recv, dev):
        return pltpu.make_async_remote_copy(src_ref=src, dst_ref=dst, send_sem=send, recv_sem=recv,
                                            device_id=(dev,), device_id_type=MESH)

    def item(i):
        side = lax.div(lax.rem(i + 4, 16), 8)
        t = lax.rem(i + 12, 16)
        m = side * (1 + lax.rem(t, 2)) + 3 * lax.div(i, 12)
        j = side * lax.div(t, 2) + (1 - side) * lax.rem(i, 4)
        return m, j

    def a_copies(i, slot):
        m, j = item(i)
        first = chip_dyn(m) * (2 * CHUNK * CHUNKS) + j * CHUNK
        for h in (0, 1):
            cols = pl.ds(pl.multiple_of(first + h * CHUNK * CHUNKS, CHUNK), CHUNK)
            yield pltpu.make_async_copy(a_hbm.at[:, cols], ring.at[slot, h], a_sem.at[slot, h])

    def own_copies(p, j):
        g, q = bufs[p].at[me, j], p % 2
        return [rcopy(g, g, isend.at[q, 0, j], irecv.at[q, 0, j], to_x),
                rcopy(g, g, isend.at[q, 1, j], irecv.at[q, 1, j], to_y),
                rcopy(g, g, dsend.at[q, 0, j], drecv.at[q, 0, j], partner)]

    def relay_x(p, j):
        g, q, half = bufs[p], p % 2, bufs[p].shape[2] // 2
        g = g.at[to_y, j, pl.ds(0, half)]
        return rcopy(g, g, isend.at[q, 2, j], irecv.at[q, 2, j], to_x)

    def relay_y(p, j):
        g, q, half = bufs[p], p % 2, bufs[p].shape[2] // 2
        g = g.at[to_x, j, pl.ds(half, half)]
        return rcopy(g, g, isend.at[q, 3, j], irecv.at[q, 3, j], to_y)

    def forward(p, m, j):
        g, q = bufs[p].at[chip_of(m) * 2 + core, j], p % 2
        return rcopy(g, g, dsend.at[q, m, j], drecv.at[q, m, j], partner)

    def arrive_xy(p, j):
        q = p % 2
        g = bufs[p].at[to_x, j]
        rcopy(g, g, isend.at[q, 0, j], irecv.at[q, 0, j], to_x).wait_recv()
        relay_y(p, j).start()
        forward(p, 1, j).start()
        g = bufs[p].at[to_y, j]
        rcopy(g, g, isend.at[q, 1, j], irecv.at[q, 1, j], to_y).wait_recv()
        relay_x(p, j).start()
        forward(p, 2, j).start()

    def arrive_d(p, j):
        q, half = p % 2, bufs[p].shape[2] // 2
        g = bufs[p].at[to_d, j, pl.ds(0, half)]
        rcopy(g, g, isend.at[q, 2, j], irecv.at[q, 2, j], to_x).wait_recv()
        g = bufs[p].at[to_d, j, pl.ds(half, half)]
        rcopy(g, g, isend.at[q, 3, j], irecv.at[q, 3, j], to_y).wait_recv()
        forward(p, 3, j).start()

    def arrive_core(p, m, j):
        q = p % 2
        g = bufs[p].at[chip_dyn(m) * 2 + 1 - core, j]
        rcopy(g, g, dsend.at[q, m, j], drecv.at[q, m, j], partner).wait_recv()

    def wait_sends(p, j):
        for copy in own_copies(p, j) + [relay_x(p, j), relay_y(p, j)] + [forward(p, m, j) for m in (1, 2, 3)]:
            copy.wait_send()

    peers = [chip_of(m) * 2 + lax.rem(core + c, 2) for m, c in ((3, 0), (3, 1), (1, 0), (1, 1), (2, 0), (2, 1), (0, 1))]

    def tile_copies(buf, send, recv):
        return [rcopy(buf.at[me], buf.at[me], send.at[k], recv.at[k], dev) for k, dev in enumerate(peers)]

    def slice_copies(src, dst, send, recv):
        return [rcopy(src.at[dev], dst.at[me], send.at[k], recv.at[k], dev) for k, dev in enumerate(peers)]

    def wait_tiles(copies, buf, send, recv):
        for k, dev in enumerate(peers):
            copies[k].wait_send()
            rcopy(buf.at[dev], buf.at[dev], send.at[k], recv.at[k], dev).wait_recv()

    sum_a = rcopy(s2.at[1 - core], ta, rsend.at[0], rrecv.at[0], partner)
    sum_b = [rcopy(hb.at[chip_of(m)], tb.at[m - 1], rsend.at[m], rrecv.at[m], chip_of(m) * 2 + core) for m in (1, 2, 3)]
    sum_c = [rcopy(s2.at[core, chip], s2.at[core, chip], rsend.at[3 + m], rrecv.at[3 + m], chip_of(m) * 2 + core)
             for m in (1, 2, 3)]
    sum_d = rcopy(s2.at[core], tc.at[core], rsend.at[7], rrecv.at[7], partner)

    def sum_two():
        sum_a.wait()
        hb[...] = s2[core] + ta[...]

    def sum_three():
        for copy in sum_b:
            copy.start()

    def sum_four():
        for copy in sum_b:
            copy.wait()
        s2[core, chip] = hb[chip] + tb[0] + tb[1] + tb[2]
        for copy in sum_c:
            copy.start()

    def sum_five():
        for m, copy in enumerate(sum_c, 1):
            copy.wait_send()
            g = s2.at[core, chip_of(m)]
            rcopy(g, g, rsend.at[3 + m], rrecv.at[3 + m], chip_of(m) * 2 + core).wait_recv()
        sum_d.start()
        tc[core] = s2[core]

    def sum_last():
        sum_d.wait_send()
        rcopy(tc.at[1 - core], tc.at[1 - core], rsend.at[7], rrecv.at[7], partner).wait_recv()

    barrier = pltpu.get_barrier_semaphore()
    for dev in peers:
        pl.semaphore_signal(barrier, inc=1, device_id=(dev,), device_id_type=MESH)
    x_copies = [pltpu.make_async_copy(x_hbm.at[j], xg.at[me, j], x_sem.at[j]) for j in range(CHUNKS)]
    small = [pltpu.make_async_copy(src, dst, w_sem.at[k]) for k, (src, dst) in enumerate(
        ((w1_hbm, w1_ref), (w2_hbm, w2_ref), (lab_hbm, lab_ref), (mask_hbm, mask_ref)))]
    for copy in x_copies + small:
        copy.start()
    for s in range(SLOTS):
        for copy in a_copies(jnp.int32(s), s):
            copy.start()
    cnt[me] = jnp.zeros(cnt.shape[1:], F32)
    los[me] = jnp.zeros(los.shape[1:], F32)
    pl.semaphore_wait(barrier, len(peers))
    for j, copy in enumerate(x_copies):
        copy.wait()
        for send in own_copies(0, j):
            send.start()

    for copy in small:
        copy.wait()
    w1t[...] = w1_ref[...].T.astype(BF16)
    cnt[me, 0:1, :] = jnp.sum(mask_ref[...].astype(F32), axis=0)

    def operands(p, m, j):
        refs = []
        for h in (0, 1):
            dev = chip_dyn(m) * 2 + h
            if p == 0:
                lhs[h, :hidden, :] = nt(w1t[...], xg[dev, j]).astype(BF16)
                refs.append(lhs.at[h, pl.ds(0, hidden)])
            elif p == 1:
                lhs[h] = nn(w2t[...], hg[dev, j]).astype(BF16)
                refs.append(lhs.at[h])
            else:
                refs.append(bufs[p].at[dev, j])
        return refs

    def product(refs, slot, rc):
        rows = pl.ds(rc * CHUNK, CHUNK) if isinstance(rc, int) else pl.ds(pl.multiple_of(rc * CHUNK, CHUNK), CHUNK)
        return nt(refs[0][...], ring[slot, 0, rows, :]) + nt(refs[1][...], ring[slot, 1, rows, :])

    def finish_one(rc):
        z = acc1[rc]
        hg[me, rc] = jnp.maximum(z, 0.0).astype(BF16)

    def finish_two(rc):
        for b in range(CHUNK // LANES):
            lanes = pl.ds(b * LANES, LANES)
            z = acc2[rc, :, lanes]
            index = lax.broadcasted_iota(jnp.int32, z.shape, 0)
            z = jnp.where(index < classes, z, -jnp.inf)
            top = jnp.max(z, axis=0, keepdims=True)
            e = jnp.exp(z - top)
            total = jnp.sum(e, axis=0, keepdims=True)
            hit = index == lab_ref[rc, :, lanes]
            picked = jnp.sum(jnp.where(hit, z, 0.0), axis=0, keepdims=True)
            mask_f = mask_ref[rc, :, lanes].astype(F32)
            los[me, 0:1, lanes] += mask_f * (jnp.log(total) + top - picked)
            onehot = jnp.where(hit, 1.0, 0.0)
            gg[me, rc, :, lanes] = ((e * (1.0 / total) - onehot) * (mask_f / mrow[:, lanes])).astype(BF16)

    def finish_three(rc):
        e2[rc, :rows_p, :] = acc2[rc].astype(BF16)
        dz = nn(w2b[...], e2[rc])
        dg[me, rc] = jnp.where(acc1[rc] > 0.0, dz, 0.0).astype(BF16)

    def finish_four(rc):
        return nt(xt[rc], acc1[rc].astype(BF16))

    def phase(p):
        acc = (acc1, acc2, acc2, acc1)[p]

        if p == 0:
            for copy in tile_copies(cnt, csend, crecv):
                copy.start()
            w2t[...] = jnp.zeros_like(w2t)
            w2t[:classes] = w2_ref[...].astype(BF16)
            wide = jnp.concatenate([w2t[...].astype(F32), jnp.zeros((w2b.shape[1] - rows_p, hidden), F32)], axis=0)
            w2b[...] = wide.T.astype(BF16)
            e2[:, rows_p:, :] = jnp.zeros((CHUNKS, e2.shape[1] - rows_p, CHUNK), BF16)
        if p == 1:
            wait_tiles(tile_copies(cnt, csend, crecv), cnt, csend, crecv)
            total = jnp.sum(jnp.sum(cnt[...], axis=0), axis=0, keepdims=True)
            mrow[...] = jnp.broadcast_to(jnp.sum(total, axis=1, keepdims=True), mrow.shape)
        if p == 2:
            for copy in tile_copies(los, lsend, lrecv):
                copy.start()
        if p == 3:
            grad = nt(e2[0], hg[me, 0])
            for rc in range(1, CHUNKS):
                grad = grad + nt(e2[rc], hg[me, rc])
            step2 = s2.shape[2]
            for k in range(8):
                s2[k // 4, k % 4] = grad[k * step2:(k + 1) * step2]
            sum_a.start()
            for rc in range(CHUNKS):
                xt[rc] = xg[me, rc].astype(F32).T.astype(BF16)
        acc[...] = jnp.zeros_like(acc)

        def step(i, carry):
            m, j = item(i)
            slot = lax.rem(i + p * ITEMS, SLOTS)

            if p > 0:
                @pl.when(i < 4)
                def _():
                    wait_sends(p - 1, i)

            arrive_core(p, m, j)
            for copy in a_copies(i, slot):
                copy.wait()
            refs = operands(p, m, j)
            acc[0] += product(refs, slot, 0)

            @pl.when((i >= 3) & (i < 11) & (lax.rem(i, 2) == 1))
            def _():
                arrive_xy(p, lax.div(i - 3, 2))

            @pl.when(i >= 11)
            def _():
                arrive_d(p, i - 11)

            if p == 3:
                pl.when(i == 4)(sum_two)
                pl.when(i == 10)(sum_three)

            for rc in range(1, CHUNKS):
                acc[rc] += product(refs, slot, rc)

            def prefetch():
                for copy in a_copies(lax.rem(i + SLOTS, ITEMS), slot):
                    copy.start()

            if p < 3:
                prefetch()
            else:
                pl.when(i + SLOTS < ITEMS)(prefetch)
            return carry

        lax.fori_loop(0, ITEMS - 1, step, 0)

        i = jnp.int32(ITEMS - 1)
        slot = (ITEMS - 1 + p * ITEMS) % SLOTS
        arrive_core(p, jnp.int32(3), CHUNKS - 1)
        for copy in a_copies(i, slot):
            copy.wait()
        refs = operands(p, jnp.int32(3), CHUNKS - 1)

        def finish(rc, carry):
            acc[rc] += product(refs, slot, rc)
            if p < 3:
                (finish_one, finish_two, finish_three)[p](rc)
                for copy in own_copies(p + 1, rc):
                    copy.start()
                return carry
            return carry + finish_four(rc)

        out = lax.fori_loop(0, CHUNKS, finish, jnp.zeros(dw1_ref.shape, F32) if p == 3 else 0)
        if p < 3:
            for copy in a_copies(jnp.int32((ITEMS - 1 + SLOTS) % ITEMS), slot):
                copy.start()
        return out

    for p in range(4):
        out = phase(p)

    step1, step2 = d1.shape[1], s2.shape[2]
    for k in range(8):
        d1[k] = out[k * step1:(k + 1) * step1]
    parts = slice_copies(d1, r1, p1send, p1recv)
    for copy in parts:
        copy.start()
    r1[me] = d1[me]
    sum_four()
    wait_tiles(tile_copies(los, lsend, lrecv), los, lsend, lrecv)
    total = jnp.sum(jnp.sum(los[...], axis=0), axis=0, keepdims=True)
    loss_ref[...] = jnp.sum(total, axis=1, keepdims=True) / mrow[:, 0:1]
    wait_tiles(parts, r1, p1send, p1recv)
    f1[me] = jnp.sum(r1[...], axis=0)
    whole = tile_copies(f1, f1send, f1recv)
    for copy in whole:
        copy.start()
    sum_five()
    for j in range(CHUNKS):
        wait_sends(3, j)
    sum_last()
    for k in range(8):
        n = min(step2, classes - k * step2)
        dw2_ref[k * step2:k * step2 + n, :] = tc[k // 4, k % 4, :n, :]
    wait_tiles(whole, f1, f1send, f1recv)
    for k in range(8):
        dw1_ref[k * step1:(k + 1) * step1, :] = f1[k]


def solution(mesh):
    axis = mesh.axis_names[0]

    def local_step(adj_rows, feat_rows, w_one, w_two, label_rows, mask_rows):
        f_in, hidden = w_one.shape
        classes = w_two.shape[1]
        rows_p = -(-classes // 32) * 32
        lanes_p = -(-classes // LANES) * LANES
        rows = adj_rows.shape[0]
        dma = pltpu.SemaphoreType.DMA
        vmem = pl.BlockSpec(memory_space=pltpu.VMEM)
        hbm = pl.BlockSpec(memory_space=pl.ANY)
        loss, dw1, dw2 = pl.pallas_call(
            functools.partial(gcn_kernel, axis, classes),
            name="gcn_step",
            out_shape=(jax.ShapeDtypeStruct((1, 1), F32), jax.ShapeDtypeStruct((f_in, hidden), F32),
                       jax.ShapeDtypeStruct((classes, hidden), F32)),
            in_specs=[hbm] * 6,
            out_specs=(vmem, vmem, vmem),
            scratch_shapes=[
                pltpu.VMEM((SLOTS, 2, rows, CHUNK), BF16),
                pltpu.VMEM((8, CHUNKS, CHUNK, f_in), BF16),
                pltpu.VMEM((8, CHUNKS, hidden, CHUNK), BF16),
                pltpu.VMEM((8, CHUNKS, rows_p, CHUNK), BF16),
                pltpu.VMEM((8, CHUNKS, hidden, CHUNK), BF16),
                pltpu.VMEM((CHUNKS, hidden, CHUNK), F32),
                pltpu.VMEM((CHUNKS, rows_p, CHUNK), F32),
                pltpu.VMEM((2, rows_p, CHUNK), BF16),
                pltpu.VMEM((CHUNKS, lanes_p, CHUNK), BF16),
                pltpu.VMEM((CHUNKS, f_in, CHUNK), BF16),
                pltpu.VMEM((f_in, hidden), F32),
                pltpu.VMEM((classes, hidden), F32),
                pltpu.VMEM((CHUNKS, 1, CHUNK), jnp.int32),
                pltpu.VMEM((CHUNKS, 1, CHUNK), jnp.int32),
                pltpu.VMEM((hidden, f_in), BF16),
                pltpu.VMEM((rows_p, hidden), BF16),
                pltpu.VMEM((hidden, lanes_p), BF16),
                pltpu.VMEM((8, 8, CHUNK), F32),
                pltpu.VMEM((8, 8, CHUNK), F32),
                pltpu.VMEM((1, CHUNK), F32),
                pltpu.VMEM((8, f_in // 8, hidden), F32),
                pltpu.VMEM((8, f_in // 8, hidden), F32),
                pltpu.VMEM((8, f_in // 8, hidden), F32),
                pltpu.VMEM((2, 4, lanes_p // 8, hidden), F32),
                pltpu.VMEM((4, lanes_p // 8, hidden), F32),
                pltpu.VMEM((2, 4, lanes_p // 8, hidden), F32),
                pltpu.VMEM((4, lanes_p // 8, hidden), F32),
                pltpu.VMEM((3, lanes_p // 8, hidden), F32),
                dma((SLOTS, 2)), dma((CHUNKS,)), dma((4,)),
                dma((2, 4, CHUNKS)), dma((2, 4, CHUNKS)), dma((2, 4, CHUNKS)), dma((2, 4, CHUNKS)),
                dma((7,)), dma((7,)), dma((7,)), dma((7,)), dma((7,)), dma((7,)), dma((7,)), dma((7,)),
                dma((8,)), dma((8,)),
            ],
            compiler_params=pltpu.CompilerParams(
                collective_id=0, has_side_effects=True, vmem_limit_bytes=67_000_000),
        )(adj_rows, feat_rows.reshape(CHUNKS, CHUNK, f_in), w_one, w_two.T,
          label_rows.reshape(CHUNKS, 1, CHUNK), mask_rows.reshape(CHUNKS, 1, CHUNK))
        return loss[0, 0], dw1, dw2.T

    return jax.shard_map(local_step, mesh=mesh, in_specs=(P(axis, None), P(axis, None), P(None, None), P(None, None), P(axis), P(axis)), out_specs=(P(), P(None, None), P(None, None)), check_vma=False)
```

time: 198 us -> 181 us (0.914)
  Pallas kernels: 191 us -> 176 us
  local copies, waits for them, and re-layouts: 6.62 us -> 3.31 us
    pallas_call x1, Pallas kernels: 191 us -> 176 us  [local_step(): pl.pallas_call(functools.partial(gcn_kernel, axis, classes), name='gcn_st...]
    unnamed x3 -> x2, local copies, waits for them, and re-layouts: 5.43 us -> 3.31 us
where the time goes in v3:
time: 181 us
  Pallas kernels  176 us (97%)
  local copies, waits for them, and re-layouts  3.31 us (2%)
  between operations  2.38 us (1%)
    pallas_call x1, Pallas kernels, local_step(): pl.pallas_call(functools.partial(gcn_kernel, axis, classes), name='gcn_st...  176 us

profile of v3, /device:TPU:0, one launch (start us, length us, event | category | flops | bytes accessed | tf_op | source)
XLA Modules:
  0.0 181.3 jit_solution(1287582383070249370)
XLA Ops:
  0.6 175.6 %gcn_step.1 = (f32[1,1]{1,0:T(1,128)}, f32[128,256]{1,0:T(8,128)}, f32[349,256]{1,0:T(8,128)}) custom-call(bf16[2048,16384]{1,0:T(8,128)(2,1)} %a_hbm.1, bf16[4,512,128]{2,1,0:T(8,128)(2,1)} %bitcast.6, f32[128,256]{1,0:T(8,128)} %w1_hbm.1, f32[349,256]{1,0:T(8,128)} %bitcast.7, s32[4,1,512]{2,1,0:T(1,128)} %bitcast.9, s32[4,1,512]{2,1,0:T(1,128)} %bitcast.10), custom_call_target="tpu_custom_call" | custom-call | tf_op jit(solution)/shard_map/gcn_step/pallas_call | solution.py:367
  176.8 1.6 copy.13
  178.4 1.7 copy.14

commit v4 on v3

--- a/solution.py
+++ b/solution.py
@@ -25,7 +25,7 @@
 
 
 def gcn_kernel(axis, classes, a_hbm, x_hbm, w1_hbm, w2_hbm, lab_hbm, mask_hbm, loss_ref, dw1_ref, dw2_ref,
-               ring, xg, hg, gg, dg, acc1, acc2, lhs, e2, xt, w1_ref, w2_ref, lab_ref, mask_ref, w1t, w2t, w2b,
+               ring, xg, hg, gg, dg, acc1, acc2, lhs, lhs2, e2, xt, w1_ref, w2_ref, lab_ref, mask_ref, w1t, w2t, w2b,
                cnt, los, mrow, d1, r1, f1, s2, ta, tc, hb, tb,
                a_sem, x_sem, w_sem, isend, irecv, dsend, drecv, csend, crecv, lsend, lrecv,
                p1send, p1recv, f1send, f1recv, rsend, rrecv):
@@ -158,7 +158,7 @@
         rcopy(tc.at[1 - core], tc.at[1 - core], rsend.at[7], rrecv.at[7], partner).wait_recv()
 
     barrier = pltpu.get_barrier_semaphore()
-    for dev in peers:
+    for dev in (to_x, to_y, partner):
         pl.semaphore_signal(barrier, inc=1, device_id=(dev,), device_id_type=MESH)
     x_copies = [pltpu.make_async_copy(x_hbm.at[j], xg.at[me, j], x_sem.at[j]) for j in range(CHUNKS)]
     small = [pltpu.make_async_copy(src, dst, w_sem.at[k]) for k, (src, dst) in enumerate(
@@ -170,7 +170,7 @@
             copy.start()
     cnt[me] = jnp.zeros(cnt.shape[1:], F32)
     los[me] = jnp.zeros(los.shape[1:], F32)
-    pl.semaphore_wait(barrier, len(peers))
+    pl.semaphore_wait(barrier, 3)
     for j, copy in enumerate(x_copies):
         copy.wait()
         for send in own_copies(0, j):
@@ -181,23 +181,28 @@
     w1t[...] = w1_ref[...].T.astype(BF16)
     cnt[me, 0:1, :] = jnp.sum(mask_ref[...].astype(F32), axis=0)
 
-    def operands(p, m, j):
-        refs = []
-        for h in (0, 1):
-            dev = chip_dyn(m) * 2 + h
-            if p == 0:
-                lhs[h, :hidden, :] = nt(w1t[...], xg[dev, j]).astype(BF16)
-                refs.append(lhs.at[h, pl.ds(0, hidden)])
-            elif p == 1:
-                lhs[h] = nn(w2t[...], hg[dev, j]).astype(BF16)
-                refs.append(lhs.at[h])
-            else:
-                refs.append(bufs[p].at[dev, j])
-        return refs
+    def prepare(p, buf, m, j, h):
+        dev = chip_dyn(m) * 2 + h
+        if p == 0:
+            buf[h, :hidden, :] = nt(w1t[...], xg[dev, j]).astype(BF16)
+        else:
+            buf[h] = nn(w2t[...], hg[dev, j]).astype(BF16)
+
+    def operands(p, buf, m, j):
+        if p == 0:
+            return [buf.at[h, pl.ds(0, hidden)] for h in (0, 1)]
+        if p == 1:
+            return [buf.at[h] for h in (0, 1)]
+        return [bufs[p].at[chip_dyn(m) * 2 + h, j] for h in (0, 1)]
 
     def product(refs, slot, rc):
         rows = pl.ds(rc * CHUNK, CHUNK) if isinstance(rc, int) else pl.ds(pl.multiple_of(rc * CHUNK, CHUNK), CHUNK)
         return nt(refs[0][...], ring[slot, 0, rows, :]) + nt(refs[1][...], ring[slot, 1, rows, :])
+
+    def label_count():
+        wait_tiles(tile_copies(cnt, csend, crecv), cnt, csend, crecv)
+        total = jnp.sum(jnp.sum(cnt[...], axis=0), axis=0, keepdims=True)
+        mrow[...] = jnp.broadcast_to(jnp.sum(total, axis=1, keepdims=True), mrow.shape)
 
     def finish_one(rc):
         z = acc1[rc]
@@ -231,17 +236,14 @@
         acc = (acc1, acc2, acc2, acc1)[p]
 
         if p == 0:
-            for copy in tile_copies(cnt, csend, crecv):
-                copy.start()
             w2t[...] = jnp.zeros_like(w2t)
             w2t[:classes] = w2_ref[...].astype(BF16)
             wide = jnp.concatenate([w2t[...].astype(F32), jnp.zeros((w2b.shape[1] - rows_p, hidden), F32)], axis=0)
             w2b[...] = wide.T.astype(BF16)
             e2[:, rows_p:, :] = jnp.zeros((CHUNKS, e2.shape[1] - rows_p, CHUNK), BF16)
         if p == 1:
-            wait_tiles(tile_copies(cnt, csend, crecv), cnt, csend, crecv)
-            total = jnp.sum(jnp.sum(cnt[...], axis=0), axis=0, keepdims=True)
-            mrow[...] = jnp.broadcast_to(jnp.sum(total, axis=1, keepdims=True), mrow.shape)
+            for copy in tile_copies(cnt, csend, crecv):
+                copy.start()
         if p == 2:
             for copy in tile_copies(los, lsend, lrecv):
                 copy.start()
@@ -257,6 +259,45 @@
                 xt[rc] = xg[me, rc].astype(F32).T.astype(BF16)
         acc[...] = jnp.zeros_like(acc)
 
+        def ready(i, slot):
+            arrive_core(p, *item(i))
+            for copy in a_copies(i, slot):
+                copy.wait()
+
+        def prefetch(i, slot):
+            for copy in a_copies(lax.rem(i + SLOTS, ITEMS), slot):
+                copy.start()
+
+        def ahead(i, buf, other):
+            slot = lax.rem(i, SLOTS)
+            arrive_core(p, *item(i + 1))
+            for copy in a_copies(i, slot):
+                copy.wait()
+            refs = operands(p, buf, *item(i))
+            for h in (0, 1):
+                prepare(p, other, *item(i + 1), h)
+            for rc in range(CHUNKS):
+                acc[rc] += product(refs, slot, rc)
+            prefetch(i, slot)
+
+        def pair(t, carry):
+            @pl.when((t >= 1) & (t <= 4))
+            def _():
+                arrive_xy(p, t - 1)
+
+            @pl.when(t >= 5)
+            def _():
+                arrive_d(p, 2 * t - 10)
+
+            ahead(2 * t, lhs, lhs2)
+
+            @pl.when(t >= 5)
+            def _():
+                arrive_d(p, 2 * t - 9)
+
+            ahead(2 * t + 1, lhs2, lhs)
+            return carry
+
         def step(i, carry):
             m, j = item(i)
             slot = lax.rem(i + p * ITEMS, SLOTS)
@@ -266,10 +307,11 @@
                 def _():
                     wait_sends(p - 1, i)
 
-            arrive_core(p, m, j)
-            for copy in a_copies(i, slot):
-                copy.wait()
-            refs = operands(p, m, j)
+            ready(i, slot)
+            if p == 1:
+                for h in (0, 1):
+                    prepare(p, lhs, m, j, h)
+            refs = operands(p, lhs, m, j)
             acc[0] += product(refs, slot, 0)
 
             @pl.when((i >= 3) & (i < 11) & (lax.rem(i, 2) == 1))
@@ -280,6 +322,9 @@
             def _():
                 arrive_d(p, i - 11)
 
+            if p == 1:
+                pl.when(i == 8)(label_count)
+
             if p == 3:
                 pl.when(i == 4)(sum_two)
                 pl.when(i == 10)(sum_three)
@@ -287,24 +332,33 @@
             for rc in range(1, CHUNKS):
                 acc[rc] += product(refs, slot, rc)
 
-            def prefetch():
-                for copy in a_copies(lax.rem(i + SLOTS, ITEMS), slot):
-                    copy.start()
-
             if p < 3:
-                prefetch()
+                prefetch(i, slot)
             else:
-                pl.when(i + SLOTS < ITEMS)(prefetch)
+                pl.when(i + SLOTS < ITEMS)(lambda: prefetch(i, slot))
             return carry
 
-        lax.fori_loop(0, ITEMS - 1, step, 0)
-
         i = jnp.int32(ITEMS - 1)
+        m, j = item(i)
         slot = (ITEMS - 1 + p * ITEMS) % SLOTS
-        arrive_core(p, jnp.int32(3), CHUNKS - 1)
-        for copy in a_copies(i, slot):
-            copy.wait()
-        refs = operands(p, jnp.int32(3), CHUNKS - 1)
+        buf = lhs
+        if p == 0:
+            arrive_core(p, *item(jnp.int32(0)))
+            for h in (0, 1):
+                prepare(p, lhs, *item(jnp.int32(0)), h)
+            lax.fori_loop(0, ITEMS // 2 - 1, pair, 0)
+            ahead(jnp.int32(ITEMS - 2), lhs, lhs2)
+            for copy in a_copies(i, slot):
+                copy.wait()
+            buf = lhs2
+        else:
+            lax.fori_loop(0, ITEMS - 1, step, 0)
+            if p == 1:
+                prepare(p, lhs, m, j, core)
+            ready(i, slot)
+            if p == 1:
+                prepare(p, lhs, m, j, 1 - core)
+        refs = operands(p, buf, m, j)
 
         def finish(rc, carry):
             acc[rc] += product(refs, slot, rc)
@@ -317,8 +371,7 @@
 
         out = lax.fori_loop(0, CHUNKS, finish, jnp.zeros(dw1_ref.shape, F32) if p == 3 else 0)
         if p < 3:
-            for copy in a_copies(jnp.int32((ITEMS - 1 + SLOTS) % ITEMS), slot):
-                copy.start()
+            prefetch(i, slot)
         return out
 
     for p in range(4):
@@ -352,6 +405,10 @@
         dw1_ref[k * step1:(k + 1) * step1, :] = f1[k]
 
 
+def output_kernel(loss_in, dw1_in, dw2_in, loss_ref, dw1_ref, dw2_ref):
+    loss_ref[...], dw1_ref[...], dw2_ref[...] = loss_in[...], dw1_in[...], dw2_in[...]
+
+
 def solution(mesh):
     axis = mesh.axis_names[0]
 
@@ -380,6 +437,7 @@
                 pltpu.VMEM((CHUNKS, hidden, CHUNK), F32),
                 pltpu.VMEM((CHUNKS, rows_p, CHUNK), F32),
                 pltpu.VMEM((2, rows_p, CHUNK), BF16),
+                pltpu.VMEM((2, hidden, CHUNK), BF16),
                 pltpu.VMEM((CHUNKS, lanes_p, CHUNK), BF16),
                 pltpu.VMEM((CHUNKS, f_in, CHUNK), BF16),
                 pltpu.VMEM((f_in, hidden), F32),
@@ -409,6 +467,9 @@
                 collective_id=0, has_side_effects=True, vmem_limit_bytes=67_000_000),
         )(adj_rows, feat_rows.reshape(CHUNKS, CHUNK, f_in), w_one, w_two.T,
           label_rows.reshape(CHUNKS, 1, CHUNK), mask_rows.reshape(CHUNKS, 1, CHUNK))
+        loss, dw1, dw2 = pl.pallas_call(
+            output_kernel, name="outputs", in_specs=[vmem] * 3, out_specs=(vmem,) * 3,
+            out_shape=tuple(jax.ShapeDtypeStruct(v.shape, v.dtype) for v in (loss, dw1, dw2)))(loss, dw1, dw2)
         return loss[0, 0], dw1, dw2.T
 
     return jax.shard_map(local_step, mesh=mesh, in_specs=(P(axis, None), P(axis, None), P(None, None), P(None, None), P(axis), P(axis)), out_specs=(P(), P(None, None), P(None, None)), check_vma=False)

time: 181 us -> 178 us (0.983)
  local copies, waits for them, and re-layouts: 3.31 us -> 0 us
    unnamed x2 -> x0, local copies, waits for them, and re-layouts: 3.31 us -> none
    pallas_call x0 -> x1, Pallas kernels: none -> 2.54 us  [local_step(): pl.pallas_call(output_kernel, name='outputs', in_specs=[vmem] * 3, out_sp...]
where the time goes in v4:
time: 178 us
  Pallas kernels  177 us (99%)
    pallas_call x1, Pallas kernels, local_step(): pl.pallas_call(functools.partial(gcn_kernel, axis, classes), name='gcn_st...  175 us

profile of v4, /device:TPU:0, one launch (start us, length us, event | category | flops | bytes accessed | tf_op | source)
XLA Modules:
  0.0 177.9 jit_solution(11189645698714927824)
XLA Ops:
  0.6 174.7 %gcn_step.1 = (f32[1,1]{1,0:T(1,128)}, f32[128,256]{1,0:T(8,128)}, f32[349,256]{1,0:T(8,128)}) custom-call(bf16[2048,16384]{1,0:T(8,128)(2,1)} %a_hbm.1, bf16[4,512,128]{2,1,0:T(8,128)(2,1)} %bitcast.6, f32[128,256]{1,0:T(8,128)} %w1_hbm.1, f32[349,256]{1,0:T(8,128)} %bitcast.7, s32[4,1,512]{2,1,0:T(1,128)} %bitcast.8, s32[4,1,512]{2,1,0:T(1,128)} %bitcast.9), custom_call_target="tpu_custom_call" | custom-call | tf_op jit(solution)/shard_map/gcn_step/pallas_call | solution.py:424
  175.4 2.5 %outputs.1 = (f32[1,1]{1,0:T(1,128)}, f32[128,256]{1,0:T(8,128)}, f32[349,256]{1,0:T(8,128)}) custom-call(f32[1,1]{1,0:T(1,128)} %get-tuple-element.9.loss_in, f32[128,256]{1,0:T(8,128)} %get-tuple-element.10.dw1_in, f32[349,256]{1,0:T(8,128)} %get-tuple-element.11.dw2_in), custom_call_target="tpu_custom_call" | custom-call | tf_op jit(solution)/shard_map/outputs/pallas_call | solution.py:470

commit v5 on v4

--- a/solution.py
+++ b/solution.py
@@ -25,7 +25,7 @@
 
 
 def gcn_kernel(axis, classes, a_hbm, x_hbm, w1_hbm, w2_hbm, lab_hbm, mask_hbm, loss_ref, dw1_ref, dw2_ref,
-               ring, xg, hg, gg, dg, acc1, acc2, lhs, lhs2, e2, xt, w1_ref, w2_ref, lab_ref, mask_ref, w1t, w2t, w2b,
+               ring, xg, hg, gg, dg, acc1, acc2, lhs, e2, xt, w1_ref, w2_ref, lab_ref, mask_ref, w1t, w2t, w2b,
                cnt, los, mrow, d1, r1, f1, s2, ta, tc, hb, tb,
                a_sem, x_sem, w_sem, isend, irecv, dsend, drecv, csend, crecv, lsend, lrecv,
                p1send, p1recv, f1send, f1recv, rsend, rrecv):
@@ -168,7 +168,6 @@
     for s in range(SLOTS):
         for copy in a_copies(jnp.int32(s), s):
             copy.start()
-    cnt[me] = jnp.zeros(cnt.shape[1:], F32)
     los[me] = jnp.zeros(los.shape[1:], F32)
     pl.semaphore_wait(barrier, 3)
     for j, copy in enumerate(x_copies):
@@ -179,20 +178,25 @@
     for copy in small:
         copy.wait()
     w1t[...] = w1_ref[...].T.astype(BF16)
-    cnt[me, 0:1, :] = jnp.sum(mask_ref[...].astype(F32), axis=0)
-
-    def prepare(p, buf, m, j, h):
+    marks = jnp.sum(mask_ref[...].astype(F32), axis=0)
+    cnt[me] = sum(marks[:, b * LANES:(b + 1) * LANES] for b in range(CHUNK // LANES))
+
+    def place(i_parity, m, j, h):
         dev = chip_dyn(m) * 2 + h
+        return (dg if i_parity == 0 else gg).at[dev, j, pl.ds(0, hidden)]
+
+    def prepare_one(i_parity, m, j):
+        for h in (0, 1):
+            place(i_parity, m, j, h)[...] = nt(w1t[...], xg[chip_dyn(m) * 2 + h, j]).astype(BF16)
+
+    def prepare_two(m, j, h):
+        lhs[h] = nn(w2t[...], hg[chip_dyn(m) * 2 + h, j]).astype(BF16)
+
+    def operands(p, i_parity, m, j):
         if p == 0:
-            buf[h, :hidden, :] = nt(w1t[...], xg[dev, j]).astype(BF16)
-        else:
-            buf[h] = nn(w2t[...], hg[dev, j]).astype(BF16)
-
-    def operands(p, buf, m, j):
-        if p == 0:
-            return [buf.at[h, pl.ds(0, hidden)] for h in (0, 1)]
+            return [place(i_parity, m, j, h) for h in (0, 1)]
         if p == 1:
-            return [buf.at[h] for h in (0, 1)]
+            return [lhs.at[h] for h in (0, 1)]
         return [bufs[p].at[chip_dyn(m) * 2 + h, j] for h in (0, 1)]
 
     def product(refs, slot, rc):
@@ -201,7 +205,7 @@
 
     def label_count():
         wait_tiles(tile_copies(cnt, csend, crecv), cnt, csend, crecv)
-        total = jnp.sum(jnp.sum(cnt[...], axis=0), axis=0, keepdims=True)
+        total = jnp.sum(cnt[...], axis=0)
         mrow[...] = jnp.broadcast_to(jnp.sum(total, axis=1, keepdims=True), mrow.shape)
 
     def finish_one(rc):
@@ -220,7 +224,7 @@
             hit = index == lab_ref[rc, :, lanes]
             picked = jnp.sum(jnp.where(hit, z, 0.0), axis=0, keepdims=True)
             mask_f = mask_ref[rc, :, lanes].astype(F32)
-            los[me, 0:1, lanes] += mask_f * (jnp.log(total) + top - picked)
+            los[me] += mask_f * (jnp.log(total) + top - picked)
             onehot = jnp.where(hit, 1.0, 0.0)
             gg[me, rc, :, lanes] = ((e * (1.0 / total) - onehot) * (mask_f / mrow[:, lanes])).astype(BF16)
 
@@ -268,14 +272,13 @@
             for copy in a_copies(lax.rem(i + SLOTS, ITEMS), slot):
                 copy.start()
 
-        def ahead(i, buf, other):
+        def ahead(i, parity):
             slot = lax.rem(i, SLOTS)
             arrive_core(p, *item(i + 1))
             for copy in a_copies(i, slot):
                 copy.wait()
-            refs = operands(p, buf, *item(i))
-            for h in (0, 1):
-                prepare(p, other, *item(i + 1), h)
+            refs = operands(p, parity, *item(i))
+            prepare_one(1 - parity, *item(i + 1))
             for rc in range(CHUNKS):
                 acc[rc] += product(refs, slot, rc)
             prefetch(i, slot)
@@ -285,17 +288,17 @@
             def _():
                 arrive_xy(p, t - 1)
 
-            @pl.when(t >= 5)
+            @pl.when(t == 5)
             def _():
-                arrive_d(p, 2 * t - 10)
-
-            ahead(2 * t, lhs, lhs2)
-
-            @pl.when(t >= 5)
+                arrive_d(p, 0)
+
+            ahead(2 * t, 0)
+
+            @pl.when(t == 5)
             def _():
-                arrive_d(p, 2 * t - 9)
-
-            ahead(2 * t + 1, lhs2, lhs)
+                arrive_d(p, 1)
+
+            ahead(2 * t + 1, 1)
             return carry
 
         def step(i, carry):
@@ -310,8 +313,8 @@
             ready(i, slot)
             if p == 1:
                 for h in (0, 1):
-                    prepare(p, lhs, m, j, h)
-            refs = operands(p, lhs, m, j)
+                    prepare_two(m, j, h)
+            refs = operands(p, 0, m, j)
             acc[0] += product(refs, slot, 0)
 
             @pl.when((i >= 3) & (i < 11) & (lax.rem(i, 2) == 1))
@@ -338,30 +341,35 @@
                 pl.when(i + SLOTS < ITEMS)(lambda: prefetch(i, slot))
             return carry
 
-        i = jnp.int32(ITEMS - 1)
-        m, j = item(i)
-        slot = (ITEMS - 1 + p * ITEMS) % SLOTS
-        buf = lhs
+        tail = [jnp.int32(i) for i in (range(ITEMS - CHUNKS, ITEMS) if p == 0 else (ITEMS - 1,))]
+        slots = [(int(i) + p * ITEMS) % SLOTS for i in (range(ITEMS - CHUNKS, ITEMS) if p == 0 else (ITEMS - 1,))]
         if p == 0:
             arrive_core(p, *item(jnp.int32(0)))
-            for h in (0, 1):
-                prepare(p, lhs, *item(jnp.int32(0)), h)
-            lax.fori_loop(0, ITEMS // 2 - 1, pair, 0)
-            ahead(jnp.int32(ITEMS - 2), lhs, lhs2)
-            for copy in a_copies(i, slot):
-                copy.wait()
-            buf = lhs2
+            prepare_one(0, *item(jnp.int32(0)))
+            lax.fori_loop(0, (ITEMS - CHUNKS) // 2, pair, 0)
+            arrive_d(p, 2)
+            arrive_core(p, *item(tail[1]))
+            prepare_one(1, *item(tail[1]))
+            arrive_d(p, 3)
+            for k in (2, 3):
+                arrive_core(p, *item(tail[k]))
+                prepare_one(k % 2, *item(tail[k]))
+            for i, slot in zip(tail, slots):
+                for copy in a_copies(i, slot):
+                    copy.wait()
         else:
             lax.fori_loop(0, ITEMS - 1, step, 0)
             if p == 1:
-                prepare(p, lhs, m, j, core)
-            ready(i, slot)
+                prepare_two(*item(tail[0]), core)
+            ready(tail[0], slots[0])
             if p == 1:
-                prepare(p, lhs, m, j, 1 - core)
-        refs = operands(p, buf, m, j)
+                prepare_two(*item(tail[0]), 1 - core)
 
         def finish(rc, carry):
-            acc[rc] += product(refs, slot, rc)
+            for k, (i, slot) in enumerate(zip(tail, slots)):
+                term = product(operands(p, k % 2, *item(i)), slot, rc)
+                whole = term if k == 0 else whole + term
+            acc[rc] += whole
             if p < 3:
                 (finish_one, finish_two, finish_three)[p](rc)
                 for copy in own_copies(p + 1, rc):
@@ -369,10 +377,14 @@
                 return carry
             return carry + finish_four(rc)
 
-        out = lax.fori_loop(0, CHUNKS, finish, jnp.zeros(dw1_ref.shape, F32) if p == 3 else 0)
-        if p < 3:
+        if p == 3:
+            out = jnp.zeros(dw1_ref.shape, F32)
+            for rc in range(CHUNKS):
+                out = finish(rc, out)
+            return out
+        lax.fori_loop(0, CHUNKS, finish, 0)
+        for i, slot in zip(tail, slots):
             prefetch(i, slot)
-        return out
 
     for p in range(4):
         out = phase(p)
@@ -386,7 +398,7 @@
     r1[me] = d1[me]
     sum_four()
     wait_tiles(tile_copies(los, lsend, lrecv), los, lsend, lrecv)
-    total = jnp.sum(jnp.sum(los[...], axis=0), axis=0, keepdims=True)
+    total = jnp.sum(los[...], axis=0)
     loss_ref[...] = jnp.sum(total, axis=1, keepdims=True) / mrow[:, 0:1]
     wait_tiles(parts, r1, p1send, p1recv)
     f1[me] = jnp.sum(r1[...], axis=0)
@@ -437,7 +449,6 @@
                 pltpu.VMEM((CHUNKS, hidden, CHUNK), F32),
                 pltpu.VMEM((CHUNKS, rows_p, CHUNK), F32),
                 pltpu.VMEM((2, rows_p, CHUNK), BF16),
-                pltpu.VMEM((2, hidden, CHUNK), BF16),
                 pltpu.VMEM((CHUNKS, lanes_p, CHUNK), BF16),
                 pltpu.VMEM((CHUNKS, f_in, CHUNK), BF16),
                 pltpu.VMEM((f_in, hidden), F32),
@@ -447,8 +458,8 @@
                 pltpu.VMEM((hidden, f_in), BF16),
                 pltpu.VMEM((rows_p, hidden), BF16),
                 pltpu.VMEM((hidden, lanes_p), BF16),
-                pltpu.VMEM((8, 8, CHUNK), F32),
-                pltpu.VMEM((8, 8, CHUNK), F32),
+                pltpu.VMEM((8, 1, LANES), F32),
+                pltpu.VMEM((8, 1, LANES), F32),
                 pltpu.VMEM((1, CHUNK), F32),
                 pltpu.VMEM((8, f_in // 8, hidden), F32),
                 pltpu.VMEM((8, f_in // 8, hidden), F32),

time: 178 us -> 175 us (0.983)
  Pallas kernels: 177 us -> 174 us
    pallas_call x1, Pallas kernels: 175 us -> 172 us  [local_step(): pl.pallas_call(functools.partial(gcn_kernel, axis, classes), name='gcn_st...]
where the time goes in v5:
time: 175 us
  Pallas kernels  174 us (99%)
    pallas_call x1, Pallas kernels, local_step(): pl.pallas_call(functools.partial(gcn_kernel, axis, classes), name='gcn_st...  172 us

profile of v5, /device:TPU:0, one launch (start us, length us, event | category | flops | bytes accessed | tf_op | source)
XLA Modules:
  0.0 174.8 jit_solution(702449494834791848)
XLA Ops:
  0.6 171.7 %gcn_step.1 = (f32[1,1]{1,0:T(1,128)}, f32[128,256]{1,0:T(8,128)}, f32[349,256]{1,0:T(8,128)}) custom-call(bf16[2048,16384]{1,0:T(8,128)(2,1)} %a_hbm.1, bf16[4,512,128]{2,1,0:T(8,128)(2,1)} %bitcast.6, f32[128,256]{1,0:T(8,128)} %w1_hbm.1, f32[349,256]{1,0:T(8,128)} %bitcast.7, s32[4,1,512]{2,1,0:T(1,128)} %bitcast.8, s32[4,1,512]{2,1,0:T(1,128)} %bitcast.9), custom_call_target="tpu_custom_call" | custom-call | tf_op jit(solution)/shard_map/gcn_step/pallas_call | solution.py:436
  172.3 2.5 %outputs.1 = (f32[1,1]{1,0:T(1,128)}, f32[128,256]{1,0:T(8,128)}, f32[349,256]{1,0:T(8,128)}) custom-call(f32[1,1]{1,0:T(1,128)} %get-tuple-element.9.loss_in, f32[128,256]{1,0:T(8,128)} %get-tuple-element.10.dw1_in, f32[349,256]{1,0:T(8,128)} %get-tuple-element.11.dw2_in), custom_call_target="tpu_custom_call" | custom-call | tf_op jit(solution)/shard_map/outputs/pallas_call | solution.py:481

commit v6 on v5

--- a/solution.py
+++ b/solution.py
@@ -9,7 +9,7 @@
 
 MESH = pl.DeviceIdType.MESH
 F32, BF16 = jnp.float32, jnp.bfloat16
-SLOTS = 4
+SLOTS = 5
 CHUNK = 512
 CHUNKS = 4
 ITEMS = 16
@@ -291,12 +291,14 @@
             @pl.when(t == 5)
             def _():
                 arrive_d(p, 0)
+                arrive_d(p, 1)
 
             ahead(2 * t, 0)
 
             @pl.when(t == 5)
             def _():
-                arrive_d(p, 1)
+                arrive_d(p, 2)
+                arrive_d(p, 3)
 
             ahead(2 * t + 1, 1)
             return carry
@@ -312,10 +314,10 @@
 
             ready(i, slot)
             if p == 1:
-                for h in (0, 1):
-                    prepare_two(m, j, h)
+                prepare_two(m, j, 1 - core)
             refs = operands(p, 0, m, j)
-            acc[0] += product(refs, slot, 0)
+            if p != 1:
+                acc[0] += product(refs, slot, 0)
 
             @pl.when((i >= 3) & (i < 11) & (lax.rem(i, 2) == 1))
             def _():
@@ -332,8 +334,10 @@
                 pl.when(i == 4)(sum_two)
                 pl.when(i == 10)(sum_three)
 
-            for rc in range(1, CHUNKS):
+            for rc in range(0 if p == 1 else 1, CHUNKS):
                 acc[rc] += product(refs, slot, rc)
+            if p == 1:
+                prepare_two(*item(i + 1), core)
 
             if p < 3:
                 prefetch(i, slot)
@@ -347,20 +351,16 @@
             arrive_core(p, *item(jnp.int32(0)))
             prepare_one(0, *item(jnp.int32(0)))
             lax.fori_loop(0, (ITEMS - CHUNKS) // 2, pair, 0)
-            arrive_d(p, 2)
-            arrive_core(p, *item(tail[1]))
-            prepare_one(1, *item(tail[1]))
-            arrive_d(p, 3)
-            for k in (2, 3):
+            for k in (1, 2, 3):
                 arrive_core(p, *item(tail[k]))
                 prepare_one(k % 2, *item(tail[k]))
             for i, slot in zip(tail, slots):
                 for copy in a_copies(i, slot):
                     copy.wait()
         else:
+            if p == 1:
+                prepare_two(*item(jnp.int32(0)), core)
             lax.fori_loop(0, ITEMS - 1, step, 0)
-            if p == 1:
-                prepare_two(*item(tail[0]), core)
             ready(tail[0], slots[0])
             if p == 1:
                 prepare_two(*item(tail[0]), 1 - core)

time: 175 us -> 174 us (level)
  no operation moved by 1% of the time
where the time goes in v6:
time: 174 us
  Pallas kernels  174 us (100%)
    pallas_call x1, Pallas kernels, local_step(): pl.pallas_call(functools.partial(gcn_kernel, axis, classes), name='gcn_st...  171 us

profile of v6, /device:TPU:0, one launch (start us, length us, event | category | flops | bytes accessed | tf_op | source)
XLA Modules:
  0.0 174.2 jit_solution(14572732392128655301)
XLA Ops:
  0.6 171.0 %gcn_step.1 = (f32[1,1]{1,0:T(1,128)}, f32[128,256]{1,0:T(8,128)}, f32[349,256]{1,0:T(8,128)}) custom-call(bf16[2048,16384]{1,0:T(8,128)(2,1)} %a_hbm.1, bf16[4,512,128]{2,1,0:T(8,128)(2,1)} %bitcast.6, f32[128,256]{1,0:T(8,128)} %w1_hbm.1, f32[349,256]{1,0:T(8,128)} %bitcast.7, s32[4,1,512]{2,1,0:T(1,128)} %bitcast.8, s32[4,1,512]{2,1,0:T(1,128)} %bitcast.9), custom_call_target="tpu_custom_call" | custom-call | tf_op jit(solution)/shard_map/gcn_step/pallas_call | solution.py:436
  171.6 2.5 %outputs.1 = (f32[1,1]{1,0:T(1,128)}, f32[128,256]{1,0:T(8,128)}, f32[349,256]{1,0:T(8,128)}) custom-call(f32[1,1]{1,0:T(1,128)} %get-tuple-element.9.loss_in, f32[128,256]{1,0:T(8,128)} %get-tuple-element.10.dw1_in, f32[349,256]{1,0:T(8,128)} %get-tuple-element.11.dw2_in), custom_call_target="tpu_custom_call" | custom-call | tf_op jit(solution)/shard_map/outputs/pallas_call | solution.py:481

commit v7 on v6

--- a/solution.py
+++ b/solution.py
@@ -233,8 +233,8 @@
         dz = nn(w2b[...], e2[rc])
         dg[me, rc] = jnp.where(acc1[rc] > 0.0, dz, 0.0).astype(BF16)
 
-    def finish_four(rc):
-        return nt(xt[rc], acc1[rc].astype(BF16))
+    def finish_four(rc, z):
+        return nt(xt[rc], z.astype(BF16))
 
     def phase(p):
         acc = (acc1, acc2, acc2, acc1)[p]
@@ -323,7 +323,7 @@
             def _():
                 arrive_xy(p, lax.div(i - 3, 2))
 
-            @pl.when(i >= 11)
+            @pl.when((i >= 11) & (i < (ITEMS - 2 if p == 3 else ITEMS)))
             def _():
                 arrive_d(p, i - 11)
 
@@ -347,6 +347,10 @@
 
         tail = [jnp.int32(i) for i in (range(ITEMS - CHUNKS, ITEMS) if p == 0 else (ITEMS - 1,))]
         slots = [(int(i) + p * ITEMS) % SLOTS for i in (range(ITEMS - CHUNKS, ITEMS) if p == 0 else (ITEMS - 1,))]
+        def half_operand(h):
+            m, j = item(tail[0])
+            return dg.at[chip_dyn(m) * 2 + h, j]
+
         if p == 0:
             arrive_core(p, *item(jnp.int32(0)))
             prepare_one(0, *item(jnp.int32(0)))
@@ -361,21 +365,31 @@
             if p == 1:
                 prepare_two(*item(jnp.int32(0)), core)
             lax.fori_loop(0, ITEMS - 1, step, 0)
-            ready(tail[0], slots[0])
+            if p == 3:
+                arrive_d(p, CHUNKS - 1)
+                for copy in a_copies(tail[0], slots[0]):
+                    copy.wait()
+                own = half_operand(core)
+                for rc in range(CHUNKS):
+                    acc[rc] += nt(own[...], ring[slots[0], core, pl.ds(rc * CHUNK, CHUNK), :])
+                arrive_core(p, *item(tail[0]))
+            else:
+                ready(tail[0], slots[0])
             if p == 1:
                 prepare_two(*item(tail[0]), 1 - core)
 
         def finish(rc, carry):
+            if p == 3:
+                rest = ring[slots[0], 1 - core, pl.ds(rc * CHUNK, CHUNK), :]
+                return carry + finish_four(rc, acc[rc] + nt(half_operand(1 - core)[...], rest))
             for k, (i, slot) in enumerate(zip(tail, slots)):
                 term = product(operands(p, k % 2, *item(i)), slot, rc)
                 whole = term if k == 0 else whole + term
             acc[rc] += whole
-            if p < 3:
-                (finish_one, finish_two, finish_three)[p](rc)
-                for copy in own_copies(p + 1, rc):
-                    copy.start()
-                return carry
-            return carry + finish_four(rc)
+            (finish_one, finish_two, finish_three)[p](rc)
+            for copy in own_copies(p + 1, rc):
+                copy.start()
+            return carry
 
         if p == 3:
             out = jnp.zeros(dw1_ref.shape, F32)

time: 174 us -> 173 us (level)
  Pallas kernels: 174 us -> 172 us
where the time goes in v7:
time: 173 us
  Pallas kernels  172 us (99%)
    pallas_call x1, Pallas kernels, local_step(): pl.pallas_call(functools.partial(gcn_kernel, axis, classes), name='gcn_st...  170 us

profile of v7, /device:TPU:0, one launch (start us, length us, event | category | flops | bytes accessed | tf_op | source)
XLA Modules:
  0.0 173.0 jit_solution(12173721541782208559)
XLA Ops:
  0.6 169.9 %gcn_step.1 = (f32[1,1]{1,0:T(1,128)}, f32[128,256]{1,0:T(8,128)}, f32[349,256]{1,0:T(8,128)}) custom-call(bf16[2048,16384]{1,0:T(8,128)(2,1)} %a_hbm.1, bf16[4,512,128]{2,1,0:T(8,128)(2,1)} %bitcast.6, f32[128,256]{1,0:T(8,128)} %w1_hbm.1, f32[349,256]{1,0:T(8,128)} %bitcast.7, s32[4,1,512]{2,1,0:T(1,128)} %bitcast.8, s32[4,1,512]{2,1,0:T(1,128)} %bitcast.9), custom_call_target="tpu_custom_call" | custom-call | tf_op jit(solution)/shard_map/gcn_step/pallas_call | solution.py:450
  170.5 2.5 %outputs.1 = (f32[1,1]{1,0:T(1,128)}, f32[128,256]{1,0:T(8,128)}, f32[349,256]{1,0:T(8,128)}) custom-call(f32[1,1]{1,0:T(1,128)} %get-tuple-element.9.loss_in, f32[128,256]{1,0:T(8,128)} %get-tuple-element.10.dw1_in, f32[349,256]{1,0:T(8,128)} %get-tuple-element.11.dw2_in), custom_call_target="tpu_custom_call" | custom-call | tf_op jit(solution)/shard_map/outputs/pallas_call | solution.py:495
